TPU v7x, 32 devices: a whole 2x2x4 slice. The times are simulated.
32 devices in a mesh: fac: 8 (over z, y), cust: 4 (over x, core).
Axes of the slice: x: 2, y: 2, z: 4, core: 2. Of those that a mesh axis runs over, the one named last changes fastest.
Arguments:
- fac_coords: bfloat16 [4096, 128], P('fac'), may hold values from -6 to 6
- cust_coords: bfloat16 [65536, 128], P(('cust', 'fac')), may hold values from -6 to 6
- open_flags: int32 [4096], P('fac'), may hold values 0 or 1
- demand: int32 [65536], P('cust'), may hold values from 1 to 4
- fixed_cost: float32 [4096], P('fac'), may hold values from 0 to 64
- capacity: float32 [4096], P('fac'), may hold values from 32 to 128
- cap_mult: float32 [4096], P('fac'), may hold values from 0 to 0.1
- cover_mult: float32 [65536], P('cust'), may hold values from 0 to 2, as said below
Outputs:
- cover_final: float32 [65536], P('cust')
- cap_final: float32 [4096], P('fac')
- bounds: float32 [3], replicated
Inputs may be any that keep to these rules, and one draw needn't show every extreme that they name: `cover_mult`: initial coverage multipliers, all in one band of width 0.4.
All inputs are finite; a program needn't handle non-finite values. No bound on the sum of `open_flags` on one device may be relied on, other than what follows from the above.
Results may differ from a plain program's by a relative error of at most 0.0003.
Values may be sent and summed in bfloat16 or wider, within the bound.
A program may use at most 64 MiB of HBM per device.

v0:
```python
import functools
import math

import jax
import jax.numpy as jnp
from jax import lax
from jax.experimental import pallas as pl
from jax.experimental.pallas import tpu as pltpu
from jax.sharding import PartitionSpec as P

MESH = pl.DeviceIdType.MESH
ITERS = 3
TAU = 0.1
ALIGN = 16
ROWS = 256
F32 = jnp.float32
BF16 = jnp.bfloat16
VMEM = pl.BlockSpec(memory_space=pltpu.VMEM)


def split3(v):
    a = v.astype(BF16)
    r = v - a.astype(F32)
    b = r.astype(BF16)
    c = (r - b.astype(F32)).astype(BF16)
    return a, b, c


def onehot_of(open_row):
    n = open_row.shape[1]
    flags = jnp.broadcast_to(open_row.astype(F32), (16, n)).astype(BF16)
    tri = (lax.broadcasted_iota(jnp.int32, (n, n), 0) <= lax.broadcasted_iota(jnp.int32, (n, n), 1)).astype(F32).astype(BF16)
    pos = jnp.dot(flags, tri, preferred_element_type=F32)[0:1]
    pos = jnp.where(open_row > 0, pos - 1.0, -1.0).astype(jnp.int32)
    hit = lax.broadcasted_iota(jnp.int32, (n, n), 0) == pos
    return jnp.where(hit, 1.0, 0.0).astype(BF16)


def nt(a, b):
    return lax.dot_general(a, b, (((1,), (1,)), ((), ())), preferred_element_type=F32)


def pre_kernel(open_ref, fac_ref, cap_ref, mu_ref, fixed_ref, cust_ref, demand_ref, cover_ref,
               comp_ref, info_ref, cust_t_ref, hq_ref, wt_ref, lam_ref, ext_ref, shut_ref):
    n, width = fac_ref.shape
    cols = cust_ref.shape[0]
    nc, _, part = info_ref.shape
    f, c = lax.axis_index("fac"), lax.axis_index("cust")
    mine = pl.ds(pl.multiple_of(f * cols, cols), cols)
    wt_ref[...] = demand_ref[:, mine].astype(F32)
    lam_ref[...] = cover_ref[:, mine]
    opened = open_ref[...].astype(F32)
    shut = mu_ref[...]
    ext = jnp.zeros((8, 128), F32)
    lane = lax.broadcasted_iota(jnp.int32, (8, 128), 1)
    for k in range(ITERS):
        fixed = jnp.sum(opened * fixed_ref[...] - (1.0 - opened) * shut * cap_ref[...])
        ext = ext + jnp.where((lane == k) & (c == 0), fixed, 0.0)
        shut = jnp.maximum(0.0, shut - 0.1 / (k + 1))
    ext_ref[...] = ext
    shut_ref[...] = shut
    hot = onehot_of(open_ref[...])
    fac = fac_ref[...]
    comp_ref[...] = jnp.dot(hot, fac, preferred_element_type=F32).astype(BF16)
    sq = fac.astype(F32) ** 2
    s1, s2, _ = split3(sq)
    ones = jnp.ones((16, width), BF16)
    half = -0.5 * (nt(ones, s1) + nt(ones, s2))[0:1]
    rows = [jnp.ones((1, n), BF16)]
    for v in (half, mu_ref[...], cap_ref[...]):
        rows.extend(split3(v))
    rows = [r.astype(F32) for r in rows] + [jnp.zeros((6, n), F32)]
    got = nt(jnp.concatenate(rows, axis=0).astype(BF16), hot)
    rows = [got[0:1]] + [got[3 * m + 1:3 * m + 2] + got[3 * m + 2:3 * m + 3] + got[3 * m + 3:3 * m + 4] for m in range(3)]
    info = jnp.concatenate(rows + [jnp.zeros((4, n), F32)], axis=0)
    for p in range(nc):
        info_ref[p] = info[:, p * part:(p + 1) * part]
    eye = (lax.broadcasted_iota(jnp.int32, (width, width), 0) == lax.broadcasted_iota(jnp.int32, (width, width), 1)).astype(F32).astype(BF16)
    turned = nt(eye, cust_ref[...])
    cust_t_ref[...] = turned.astype(BF16)
    hq_ref[...] = 0.5 * jnp.sum(turned * turned, axis=0, keepdims=True)


def sync(peers):
    barrier = pltpu.get_barrier_semaphore()
    for peer in peers:
        pl.semaphore_signal(barrier, inc=1, device_id=peer, device_id_type=MESH)
    pl.semaphore_wait(barrier, len(peers))


def gather_kernel(nf, nc, comp_ref, info_ref, facs_ref, infos_ref, s1, r1, s2, r2, s3, r3, loc):
    f, c = lax.axis_index("fac"), lax.axis_index("cust")
    fp = [(lax.rem(f + d, nf), c) for d in range(1, nf)]
    half = nc // 2
    core = lax.rem(c, 2)
    twin = (f, c + 1 - 2 * core)
    sides = [lax.rem(c + 2 * d, nc) for d in range(1, half)]
    part = comp_ref.shape[0] // nc
    sync(fp + [(f, e) for e in sides] + [twin])

    def rows(q):
        return pl.ds(pl.multiple_of(q * part, part), part)

    def move(src, q, k, send, recv, peer, own=False):
        a = comp_ref.at[rows(q)] if own else facs_ref.at[src, rows(q)]
        b = info_ref.at[q] if own else infos_ref.at[src, q]
        pair = [
            pltpu.make_async_remote_copy(a, facs_ref.at[src, rows(q)], send.at[k, 0], recv.at[k, 0], device_id=peer, device_id_type=MESH),
            pltpu.make_async_remote_copy(b, infos_ref.at[src, q], send.at[k, 1], recv.at[k, 1], device_id=peer, device_id_type=MESH),
        ]
        for cpy in pair:
            cpy.start()
        return pair

    first = [move(f, c, d, s1, r1, peer, True) for d, peer in enumerate(fp)]
    own = pltpu.make_async_copy(comp_ref, facs_ref.at[f], loc.at[0])
    own.start()
    own_info = pltpu.make_async_copy(info_ref, infos_ref.at[f], loc.at[1])
    own_info.start()
    across, over = [], []
    for d in range(nf - 1):
        src = lax.rem(f + nf - 1 - d, nf)
        for cpy in first[d]:
            cpy.wait_recv()
        for e, q in enumerate(sides):
            across.append((src, lax.rem(c + nc - 2 * (e + 1), nc), move(src, c, d * (half - 1) + e, s2, r2, (f, q))))
        over.append(move(src, c, d * half, s3, r3, twin))
        for e in range(half - 1):
            if d > 0:
                ready = across[(d - 1) * (half - 1) + e]
                for cpy in ready[2]:
                    cpy.wait_recv()
                over.append(move(ready[0], ready[1], (d - 1) * half + 1 + e, s3, r3, twin))
    for e in range(half - 1):
        ready = across[(nf - 2) * (half - 1) + e]
        for cpy in ready[2]:
            cpy.wait_recv()
        over.append(move(ready[0], ready[1], (nf - 2) * half + 1 + e, s3, r3, twin))
    for pair in first + [a[2] for a in across]:
        for cpy in pair:
            cpy.wait_send()
    for pair in over:
        for cpy in pair:
            cpy.wait()
    own.wait()
    own_info.wait()


def step_kernel(step, facs_ref, infos_ref, mu_ref, load_ref, cust_t_ref, hq_ref, lam_ref, wt_ref, ext_ref,
                part_ref, mu_out_ref, lam_out_ref, tot_ref,
                info_ref, a_ref, w_ref, y_ref, x_ref, d_ref, acc_ref, cov_ref, soft_ref):
    first, size, prev = step == 0, 0.1 / (step + 1), 0.1 / max(step, 1)
    nf, n, width = facs_ref.shape
    cols = cust_t_ref.shape[1]
    block = y_ref.shape[2]
    tiles = cols // block
    lam = lam_ref[...]
    wt = wt_ref[...]
    a1, a2, a3 = split3(64.0 * lam - hq_ref[...])
    one_c = jnp.ones((3, cols), F32)
    mw = jnp.broadcast_to(-64.0 * wt, (3, cols))
    aug = jnp.concatenate([a1.astype(F32), a2.astype(F32), a3.astype(F32), one_c, mw, jnp.zeros((7, cols), F32)], axis=0)
    w_ref[0:width, :] = cust_t_ref[...]
    w_ref[width:width + 16, :] = aug.astype(BF16)
    w_ref[width + 16:, :] = jnp.zeros((width - 16, cols), BF16)
    cov_ref[...] = jnp.zeros_like(cov_ref)
    soft_ref[...] = jnp.zeros_like(soft_ref)
    lane = lax.broadcasted_iota(jnp.int32, (ROWS, width), 1)
    pad = jnp.where(lane == 3, -30000.0, 0.0).astype(BF16)
    sel = (lax.broadcasted_iota(jnp.int32, (16, width), 0) == lax.broadcasted_iota(jnp.int32, (16, width), 1)).astype(F32).astype(BF16)
    top = (lax.broadcasted_iota(jnp.int32, (16, 128), 0) == 0).astype(F32).astype(BF16)
    wrows = jnp.concatenate([wt, jnp.zeros((15, cols), F32)], axis=0).astype(BF16)
    d_ref[...] = lax.dot_general(wrows, top, (((0,), (0,)), ((), ())), preferred_element_type=F32).astype(BF16)
    nc, part = infos_ref.shape[1], infos_ref.shape[3]
    for f in range(nf):
        info_ref[f] = jnp.concatenate([infos_ref[f, p] for p in range(nc)], axis=1)
    offs = []
    off = jnp.int32(0)
    one_r = jnp.ones((3, n), F32)
    for f in range(nf):
        valid = info_ref[f, 0:1, :]
        cap = info_ref[f, 3:4, :]
        if first:
            mu = info_ref[f, 2:3, :]
        else:
            mu = mu_ref[f:f + 1, :]
            load = load_ref[f:f + 1, :]
            mu = jnp.maximum(0.0, mu + prev * (load - cap) / (load + jnp.where(valid > 0, cap, 1.0)))
        mu = mu * valid
        mu_out_ref[f:f + 1, :] = mu
        b = jnp.where(valid > 0, info_ref[f, 1:2, :], -30000.0)
        parts = [p.astype(F32) for p in split3(b) + split3(mu)]
        rows = jnp.concatenate([one_r] + parts + [jnp.zeros((7, n), F32)], axis=0).astype(BF16)
        side = lax.dot_general(rows, sel, (((0,), (0,)), ((), ())), preferred_element_type=F32).astype(BF16)
        count = jnp.sum(valid).astype(jnp.int32)
        off = pl.multiple_of(off, ALIGN)
        offs.append(off)
        a_ref[pl.ds(off, n), 0:width] = facs_ref[f]
        a_ref[pl.ds(off, n), width:2 * width] = side
        off = off + ((count + ALIGN - 1) // ALIGN) * ALIGN
    tail = pl.multiple_of(off, ALIGN)
    a_ref[pl.ds(tail, ROWS), 0:width] = jnp.zeros((ROWS, width), BF16)
    a_ref[pl.ds(tail, ROWS), width:2 * width] = pad
    n_blocks = (off + ROWS - 1) // ROWS
    scale = math.log2(math.e) / 6.4

    def body(i, _):
        base = pl.multiple_of(i * ROWS, ROWS)
        lhs = a_ref[pl.ds(base, ROWS), :]

        def dot(t):
            y_ref[t % 2] = jnp.dot(lhs, w_ref[:, t * block:(t + 1) * block], preferred_element_type=F32)

        dot(0)
        for t in range(tiles):
            if t + 1 < tiles:
                dot(t + 1)
            covs = [cov_ref[:, t * block + q * 128:t * block + (q + 1) * 128] for q in range(block // 128)]
            softs = [soft_ref[:, t * block + q * 128:t * block + (q + 1) * 128] for q in range(block // 128)]
            for r in range(0, ROWS, 32):
                for q in range(block // 128):
                    es = [jnp.exp2(y_ref[t % 2, r + 8 * s:r + 8 * s + 8, q * 128:(q + 1) * 128] * scale) for s in range(4)]
                    us = [1.0 + e for e in es]
                    p01 = us[0] * us[1]
                    p23 = us[2] * us[3]
                    r01 = 1.0 / p01
                    r23 = 1.0 / p23
                    xs = [es[0] * (us[1] * r01), es[1] * (us[0] * r01), es[2] * (us[3] * r23), es[3] * (us[2] * r23)]
                    covs[q] = covs[q] + ((xs[0] + xs[1]) + (xs[2] + xs[3]))
                    softs[q] = softs[q] + jnp.log(p01 * p23)
                    for h in range(2):
                        both = jnp.concatenate([xs[2 * h], xs[2 * h + 1]], axis=0).astype(BF16)
                        x_ref[t % 2, r + 16 * h:r + 16 * h + 16, q * 128:(q + 1) * 128] = both
            got = jnp.dot(x_ref[t % 2], d_ref[t * block:(t + 1) * block, :], preferred_element_type=F32)
            at = pl.ds(base, ROWS)
            acc_ref[at, :] = got if t == 0 else acc_ref[at, :] + got
            for q in range(block // 128):
                cov_ref[:, t * block + q * 128:t * block + (q + 1) * 128] = covs[q]
                soft_ref[:, t * block + q * 128:t * block + (q + 1) * 128] = softs[q]
        return 0

    lax.fori_loop(0, n_blocks, body, 0)
    diag = lax.broadcasted_iota(jnp.int32, (128, 128), 0) == lax.broadcasted_iota(jnp.int32, (128, 128), 1)
    for f in range(nf):
        for b in range(n // 128):
            at = pl.ds(pl.multiple_of(offs[f] + b * 128, ALIGN), 128)
            got = jnp.sum(jnp.where(diag, acc_ref[at, :], 0.0), axis=0, keepdims=True)
            part_ref[f:f + 1, b * 128:(b + 1) * 128] = jnp.where(info_ref[f, 0:1, b * 128:(b + 1) * 128] > 0, got, 0.0)
    cover = jnp.sum(cov_ref[...], axis=0, keepdims=True)
    soft = jnp.sum(soft_ref[...], axis=0, keepdims=True)
    me, c = lax.axis_index("fac"), lax.axis_index("cust")
    mine = jnp.sum(mu_out_ref[pl.ds(me, 1), :] * info_ref[me, 3:4, :])
    here = jnp.sum(wt * lam - TAU * wt * soft) - jnp.where(c == 0, mine, 0.0)
    spot = lax.broadcasted_iota(jnp.int32, (8, 128), 1) == step
    tot = ext_ref[...] + jnp.where(spot, here, 0.0)
    tot_ref[...] = tot
    if part_ref.shape[0] > nf:
        part_ref[nf:nf + 8, :] = jnp.zeros((8, n), F32)
        part_ref[nf:nf + 8, 0:128] = tot
    lam_out_ref[...] = lam + size * wt * (1.0 - cover) / (1.0 + cover)


def exchange(peers, src, slots, send, recv):
    copies = []
    for d, peer in enumerate(peers):
        cpy = pltpu.make_async_remote_copy(src, slots.at[d], send.at[d], recv.at[d], device_id=peer, device_id_type=MESH)
        cpy.start()
        copies.append(cpy)
    return copies


def reduce_kernel(nf, nc, x_ref, lam_ref, out_ref, lam_out, got1, mid, got2, s1, r1, s2, r2, s3, r3, loc):
    f, c = lax.axis_index("fac"), lax.axis_index("cust")
    fp = [(lax.rem(f + d, nf), c) for d in range(1, nf)]
    cp = [(f, lax.rem(c + d, nc)) for d in range(1, nc)]
    sync(fp + cp)
    first = exchange(cp, x_ref, got1, s1, r1)
    lams = []
    if lam_ref is not None:
        own = pltpu.make_async_copy(lam_ref, lam_out.at[f], loc)
        own.start()
        for d, peer in enumerate(fp):
            cpy = pltpu.make_async_remote_copy(lam_ref, lam_out.at[f], s3.at[d], r3.at[d], device_id=peer, device_id_type=MESH)
            cpy.start()
            lams.append(cpy)
    total = x_ref[...]
    for d, cpy in enumerate(first):
        cpy.wait()
        total = total + got1[d]
    mid[...] = total
    second = exchange(fp, mid, got2, s2, r2)
    for d, cpy in enumerate(second):
        cpy.wait()
        total = total + got2[d]
    out_ref[...] = total
    for cpy in lams:
        cpy.wait()
    if lam_ref is not None:
        own.wait()


def reduce_plain(nf, nc, x_ref, out_ref, got1, mid, got2, s1, r1, s2, r2):
    reduce_kernel(nf, nc, x_ref, None, out_ref, None, got1, mid, got2, s1, r1, s2, r2, None, None, None)


def finish_kernel(total_cust, total_ref, mu_ref, infos_ref, open_ref, shut_ref, out_ref, bound_ref):
    nf, nc = infos_ref.shape[0:2]
    n = open_ref.shape[1]
    f = lax.axis_index("fac")
    load = total_ref[pl.ds(f, 1), :]
    cap = jnp.concatenate([infos_ref[f, p, 3:4, :] for p in range(nc)], axis=1)
    new = jnp.maximum(0.0, mu_ref[pl.ds(f, 1), :] + (0.1 / ITERS) * (load - cap) / (load + jnp.where(cap > 0, cap, 1.0)))
    rows = jnp.concatenate([v.astype(F32) for v in split3(new)] + [jnp.zeros((13, n), F32)], axis=0).astype(BF16)
    got = jnp.dot(rows, onehot_of(open_ref[...]), preferred_element_type=F32)
    out_ref[...] = jnp.where(open_ref[...] > 0, got[0:1] + got[1:2] + got[2:3], shut_ref[...])
    bound_ref[...] = total_ref[nf:nf + 1, 0:128] / total_cust


def params(cid=None, mib=56):
    return pltpu.CompilerParams(collective_id=cid, has_side_effects=True, vmem_limit_bytes=mib * 2 ** 20) if cid is not None else pltpu.CompilerParams(vmem_limit_bytes=mib * 2 ** 20)


def local(nf, nc, fac_coords, cust_coords, open_flags, demand, fixed_cost, capacity, cap_mult, cover_mult):
    n, width = fac_coords.shape
    cols = cust_coords.shape[0]
    total_cust = cols * nf * nc
    sd = jax.ShapeDtypeStruct
    dma = pltpu.SemaphoreType.DMA
    part = n // nc
    open_row = open_flags.reshape(1, n)
    comp, info, cust_t, hq, wt, lam, ext, shut = pl.pallas_call(
        pre_kernel,
        out_shape=(sd((n, width), BF16), sd((nc, 8, part), F32), sd((width, cols), BF16), sd((1, cols), F32),
                   sd((1, cols), F32), sd((1, cols), F32), sd((8, 128), F32), sd((1, n), F32)),
        in_specs=[VMEM] * 8, out_specs=(VMEM,) * 8, compiler_params=params(), name="pre",
    )(open_row, fac_coords, capacity.reshape(1, n), cap_mult.reshape(1, n), fixed_cost.reshape(1, n), cust_coords,
      demand.reshape(1, nf * cols), cover_mult.reshape(1, nf * cols))
    sides = (nf - 1) * (nc // 2 - 1)
    facs, infos = pl.pallas_call(
        functools.partial(gather_kernel, nf, nc),
        out_shape=(sd((nf, n, width), BF16), sd((nf, nc, 8, part), F32)),
        in_specs=[VMEM] * 2, out_specs=(VMEM,) * 2,
        scratch_shapes=[dma((nf - 1, 2)), dma((nf - 1, 2)), dma((sides, 2)), dma((sides, 2)),
                        dma(((nf - 1) * (nc // 2), 2)), dma(((nf - 1) * (nc // 2), 2)), dma((2,))],
        compiler_params=params(0), name="gather",
    )(comp, info)
    block = math.gcd(cols, 512)
    total_rows = nf * n
    mu = load = hq
    tot = ext
    for step in range(ITERS):
        last = step == ITERS - 1
        rows = nf + 8 if last else nf
        payload, mu, lam, tot = pl.pallas_call(
            functools.partial(step_kernel, step),
            out_shape=(sd((rows, n), F32), sd((nf, n), F32), sd((1, cols), F32), sd((8, 128), F32)),
            in_specs=[VMEM] * 9, out_specs=(VMEM,) * 4,
            scratch_shapes=[
                pltpu.VMEM((nf, 8, n), F32),
                pltpu.VMEM((total_rows + n + ROWS, 2 * width), BF16),
                pltpu.VMEM((2 * width, cols), BF16),
                pltpu.VMEM((2, ROWS, block), F32),
                pltpu.VMEM((2, ROWS, block), BF16),
                pltpu.VMEM((cols, 128), BF16),
                pltpu.VMEM((total_rows + n + ROWS, 128), F32),
                pltpu.VMEM((8, cols), F32),
                pltpu.VMEM((8, cols), F32),
            ],
            compiler_params=params(), name="step",
        )(facs, infos, mu, load, cust_t, hq, lam, wt, tot)
        scratch = [pltpu.VMEM((nc - 1, rows, n), F32), pltpu.VMEM((rows, n), F32), pltpu.VMEM((nf - 1, rows, n), F32),
                   dma((nc - 1,)), dma((nc - 1,)), dma((nf - 1,)), dma((nf - 1,))]
        if not last:
            load = pl.pallas_call(
                functools.partial(reduce_plain, nf, nc),
                out_shape=sd((rows, n), F32), in_specs=[VMEM], out_specs=VMEM,
                scratch_shapes=scratch, compiler_params=params(1 + step), name="reduce",
            )(payload)
        else:
            load, lam_all = pl.pallas_call(
                functools.partial(reduce_kernel, nf, nc),
                out_shape=(sd((rows, n), F32), sd((nf, 1, cols), F32)), in_specs=[VMEM] * 2, out_specs=(VMEM,) * 2,
                scratch_shapes=scratch + [dma((nf - 1,)), dma((nf - 1,)), dma(())],
                compiler_params=params(1 + step), name="reduce",
            )(payload, lam)
    cap_final, bounds = pl.pallas_call(
        functools.partial(finish_kernel, total_cust), out_shape=(sd((1, n), F32), sd((1, 128), F32)),
        in_specs=[VMEM] * 5, out_specs=(VMEM,) * 2, compiler_params=params(), name="finish",
    )(load, mu, infos, open_row, shut)
    return lam_all.reshape(nf * cols), cap_final.reshape(n), bounds[0, :ITERS]


def solution(mesh):
    nf, nc = mesh.shape["fac"], mesh.shape["cust"]
    return jax.shard_map(
        functools.partial(local, nf, nc),
        mesh=mesh,
        in_specs=(P("fac", None), P(("cust", "fac"), None), P("fac"), P("cust"), P("fac"), P("fac"), P("fac"), P("cust")),
        out_specs=(P("cust"), P("fac"), P()),
        check_vma=False,
    )
```

profile of v0, /device:TPU:0, one launch (start us, length us, event | category | flops | bytes accessed | tf_op | source)
XLA Modules:
  0.0 115.0 jit_solution(260135992715028294)
XLA Ops:
  0.6 2.8 %pre.1 = (bf16[512,128]{1,0:T(8,128)(2,1)}, f32[4,8,128]{2,1,0:T(8,128)}, bf16[128,2048]{1,0:T(8,128)(2,1)}, f32[1,2048]{1,0:T(1,128)}, f32[1,2048]{1,0:T(1,128)...) custom-call(s32[1,512]{1,0:T(1,128)} %bitcast.13, bf16[512,128]{1,0:T(8,128)(2,1)} %fac_ref.1, ...), custom_call_target="tpu_custom_call" | custom-call | tf_op jit(solution)/shard_map/pre/pallas_call | solution.py:331
  3.4 26.0 %gather.1 = (bf16[8,512,128]{2,1,0:T(8,128)(2,1)}, f32[8,4,8,128]{3,2,1,0:T(8,128)}) custom-call(bf16[512,128]{1,0:T(8,128)(2,1)} %get-tuple-element.28.comp_ref, f32[4,8,128]{2,1,0:T(8,128)} %get-tuple-element.29.info_ref), custom_call_target="tpu_custom_call" | custom-call | tf_op jit(solution)/shard_map/gather/pallas_call | solution.py:339
  29.4 14.8 %step.3 = (f32[8,512]{1,0:T(8,128)}, f32[8,512]{1,0:T(8,128)}, f32[1,2048]{1,0:T(1,128)}, f32[8,128]{1,0:T(8,128)}) custom-call(bf16[8,512,128]{2,1,0:T(8,128)(2,1)} %get-tuple-element.30.facs_ref, f32[8,4,8,128]{3,2,1,0:T(8,128)} %get-tuple-element.31.infos_ref, f32[1,2048]{1,0:T(1,128)} %get-tuple-element.32.mu_ref.load_ref.hq_ref, ...), custom_call_target="tpu_custom_call" | custom-call | tf_op jit(solution)/shard_map/step/pallas_call | solution.py:354
  44.3 11.2 %reduce.3.load_ref = f32[8,512]{1,0:T(8,128)} custom-call(f32[8,512]{1,0:T(8,128)} %get-tuple-element.38.x_ref), custom_call_target="tpu_custom_call" | custom-call | tf_op jit(solution)/shard_map/reduce/pallas_call | solution.py:374
  55.4 14.8 %step.4 = (f32[8,512]{1,0:T(8,128)}, f32[8,512]{1,0:T(8,128)}, f32[1,2048]{1,0:T(1,128)}, f32[8,128]{1,0:T(8,128)}) custom-call(bf16[8,512,128]{2,1,0:T(8,128)(2,1)} %get-tuple-element.30.facs_ref, f32[8,4,8,128]{3,2,1,0:T(8,128)} %get-tuple-element.31.infos_ref, f32[8,512]{1,0:T(8,128)} %get-tuple-element.37.mu_ref, f32[8,512]{1,0:T(8,128)} %reduce.3.load_ref, ...), custom_call_target="tpu_custom_call" | custom-call | tf_op jit(solution)/shard_map/step/pallas_call | solution.py:354
  70.3 11.6 %reduce.4.load_ref = f32[8,512]{1,0:T(8,128)} custom-call(f32[8,512]{1,0:T(8,128)} %get-tuple-element.42.x_ref), custom_call_target="tpu_custom_call" | custom-call | tf_op jit(solution)/shard_map/reduce/pallas_call | solution.py:374
  81.8 14.9 %step.5 = (f32[16,512]{1,0:T(8,128)}, f32[8,512]{1,0:T(8,128)}, f32[1,2048]{1,0:T(1,128)}, f32[8,128]{1,0:T(8,128)}) custom-call(bf16[8,512,128]{2,1,0:T(8,128)(2,1)} %get-tuple-element.30.facs_ref, f32[8,4,8,128]{3,2,1,0:T(8,128)} %get-tuple-element.31.infos_ref, f32[8,512]{1,0:T(8,128)} %get-tuple-element.41.mu_ref, f32[8,512]{1,0:T(8,128)} %reduce.4.load_ref, ...), custom_call_target="tpu_custom_call" | custom-call | tf_op jit(solution)/shard_map/step/pallas_call | solution.py:354
  96.7 14.5 %reduce.5 = (f32[16,512]{1,0:T(8,128)}, f32[8,1,2048]{2,1,0:T(1,128)}) custom-call(f32[16,512]{1,0:T(8,128)} %get-tuple-element.45.x_ref, f32[1,2048]{1,0:T(1,128)} %get-tuple-element.46.lam_ref), custom_call_target="tpu_custom_call" | custom-call | tf_op jit(solution)/shard_map/reduce/pallas_call | solution.py:380
  111.2 0.0 copy-start
  111.2 2.0 %finish.1 = (f32[1,512]{1,0:T(1,128)}, f32[1,128]{1,0:T(1,128)}) custom-call(f32[16,512]{1,0:T(8,128)} %get-tuple-element.48.total_ref, f32[8,512]{1,0:T(8,128)} %get-tuple-element.49.mu_ref, f32[8,4,8,128]{3,2,1,0:T(8,128)} %get-tuple-element.31.infos_ref, s32[1,512]{1,0:T(1,128)} %bitcast.14, f32[1,512]{1,0:T(1,128)} %get-tuple-element.50.shut_ref), custom_call_target="tpu_custom_call" | custom-call | tf_op jit(solution)/shard_map/finish/pallas_call | solution.py:386
  113.2 0.0 copy-start.1
  113.2 0.7 copy-done.1
  113.8 0.5 slice_bitcast_fusion
  114.3 0.0 copy-done
  114.4 0.6 copy.12
Async XLA Ops:
  111.2 3.1 %copy-start = (f32[8,1,2048]{2,1,0:T(1,128)S(1)}, f32[8,1,2048]{2,1,0:T(1,128)}, u32[]{:S(2)}) copy-start(f32[8,1,2048]{2,1,0:T(1,128)} %get-tuple-element.47) | copy-start | bytes 196612
  113.2 0.7 copy-start.1
where the time goes:
time: 115 us
  Pallas kernels  113 us (98%)
  local copies, waits for them, and re-layouts  1.8 us (2%)
    pallas_call x3, Pallas kernels, local(): pl.pallas_call(functools.partial(step_kernel, step), out_shape=(sd((rows,...  44.5 us
    pallas_call x1, Pallas kernels, local(): pl.pallas_call(functools.partial(gather_kernel, nf, nc), out_shape=(sd((n...  26 us
    pallas_call x2, Pallas kernels, local(): pl.pallas_call(functools.partial(reduce_plain, nf, nc), out_shape=sd((row...  22.7 us
    pallas_call x1, Pallas kernels, local(): pl.pallas_call(functools.partial(reduce_kernel, nf, nc), out_shape=(sd((r...  14.5 us
    pallas_call x1, Pallas kernels, local(): pl.pallas_call(pre_kernel, out_shape=(sd((n, width), BF16), sd((nc, 8, pa...  2.76 us

commit v1 on v0

v1 whole, which is shorter than its diff:
```python
import functools
import math

import jax
import jax.numpy as jnp
from jax import lax
from jax.experimental import pallas as pl
from jax.experimental.pallas import tpu as pltpu
from jax.sharding import PartitionSpec as P

MESH = pl.DeviceIdType.MESH
ITERS = 3
TAU = 0.1
LAG = 3
CLOSED = -30000.0
F32 = jnp.float32
BF16 = jnp.bfloat16
VMEM = pl.BlockSpec(memory_space=pltpu.VMEM)


def split3(v):
    a = v.astype(BF16)
    r = v - a.astype(F32)
    b = r.astype(BF16)
    c = (r - b.astype(F32)).astype(BF16)
    return a, b, c


def nt(a, b):
    return lax.dot_general(a, b, (((1,), (1,)), ((), ())), preferred_element_type=F32)


def eye_of(rows, width):
    hit = lax.broadcasted_iota(jnp.int32, (rows, width), 0) == lax.broadcasted_iota(jnp.int32, (rows, width), 1)
    return hit.astype(F32).astype(BF16)


def onehot_of(open_row, rows):
    n = open_row.shape[1]
    flags = jnp.broadcast_to(open_row.astype(F32), (16, n)).astype(BF16)
    tri = (lax.broadcasted_iota(jnp.int32, (n, n), 0) <= lax.broadcasted_iota(jnp.int32, (n, n), 1)).astype(F32).astype(BF16)
    pos = jnp.dot(flags, tri, preferred_element_type=F32)[0:1]
    pos = jnp.where(open_row > 0, pos - 1.0, -1.0).astype(jnp.int32)
    hit = lax.broadcasted_iota(jnp.int32, (rows, n), 0) == pos
    return jnp.where(hit, 1.0, 0.0).astype(BF16)


def solve_kernel(nf, nc, rows, total_cust,
                 open_ref, fac_ref, cap_ref, mu_in_ref, fixed_ref, cust_ref, demand_ref, cover_ref,
                 lam_out, cap_out, bound_out, flag_out,
                 facs, infos, hot_ref, side, w_ref, y_ref, acc, cov_ref, soft_ref, d_ref, hq_ref, lam_ref, mus, caps,
                 tot_ref, pay, got1, mid, got2,
                 s1, r1, s2, r2, s3, r3, s4, r4, s5, r5, s6, r6):
    f, c = lax.axis_index("fac"), lax.axis_index("cust")
    n, width = fac_ref.shape
    cols = cust_ref.shape[0]
    part = infos.shape[3]
    padded = part * nc
    wide = pay.shape[2]
    half = nc // 2
    core = lax.rem(c, 2)
    twin = (f, c + 1 - 2 * core)
    barrier = pltpu.get_barrier_semaphore()
    for d in range(1, nf):
        pl.semaphore_signal(barrier, inc=1, device_id=(lax.rem(f + d, nf), c), device_id_type=MESH)
    for d in range(1, nc):
        pl.semaphore_signal(barrier, inc=1, device_id=(f, lax.rem(c + d, nc)), device_id_type=MESH)

    opened = open_ref[...].astype(F32)
    hot = onehot_of(open_ref[...], padded)
    hot_ref[...] = hot
    fac = fac_ref[...]
    facs[f] = jnp.dot(hot, fac, preferred_element_type=F32).astype(BF16)
    q1, q2, _ = split3(fac.astype(F32) ** 2)
    ones = jnp.ones((16, width), BF16)
    halfsq = -0.5 * (nt(ones, q1) + nt(ones, q2))[0:1]
    rows16 = [jnp.ones((1, n), BF16)]
    for v in (halfsq, mu_in_ref[...], cap_ref[...]):
        rows16.extend(split3(v))
    rows16 = [r.astype(F32) for r in rows16] + [jnp.zeros((6, n), F32)]
    got = nt(jnp.concatenate(rows16, axis=0).astype(BF16), hot)
    bias = jnp.where(got[0:1] > 0, got[1:2] + got[2:3] + got[3:4], CLOSED)
    count = jnp.broadcast_to(jnp.sum(opened, axis=1, keepdims=True), (1, padded))
    info = jnp.concatenate([bias, got[4:5] + got[5:6] + got[6:7], got[7:8] + got[8:9] + got[9:10], count, jnp.zeros((4, padded), F32)], axis=0)
    for p in range(nc):
        infos[f, p] = info[:, p * part:(p + 1) * part]

    def rows_of(q):
        return pl.ds(pl.multiple_of(q * part, 16), part)

    def move(src, q, send, recv, peer):
        a, b = facs.at[src, rows_of(q)], infos.at[src, q]
        return [pltpu.make_async_remote_copy(a, a, send.at[0], recv.at[0], device_id=peer, device_id_type=MESH),
                pltpu.make_async_remote_copy(b, b, send.at[1], recv.at[1], device_id=peer, device_id_type=MESH)]

    def first_copy(src, dst, peer_f):
        return move(src, c, s1.at[dst], r1.at[src], (peer_f, c))

    def side_copy(src, e, q):
        return move(src, q, s2.at[src, e], r2.at[src, e], (f, lax.rem(c + 2 * (e + 1), nc)))

    def twin_copy(src, e, q):
        return move(src, q, s3.at[src, e], r3.at[src, e], twin)

    pl.semaphore_wait(barrier, nf + nc - 2)
    for d in sorted(range(1, nf), key=lambda v: abs(v - nf // 2)):
        peer = lax.rem(f + d, nf)
        for cpy in first_copy(f, peer, peer):
            cpy.start()

    ext = jnp.zeros((1, 128), F32)
    lane = lax.broadcasted_iota(jnp.int32, (1, 128), 1)
    shut = mu_in_ref[...]
    for k in range(ITERS):
        fixed = jnp.sum(opened * fixed_ref[...] - (1.0 - opened) * shut * cap_ref[...])
        ext = ext + jnp.where((lane == k) & (c == 0), fixed, 0.0)
        shut = jnp.maximum(0.0, shut - 0.1 / (k + 1))
    tot_ref[...] = ext
    mine = pl.ds(pl.multiple_of(f * cols, cols), cols)
    wt = demand_ref[:, mine].astype(F32)
    lam = cover_ref[:, mine]
    lam_ref[...] = lam
    d_ref[...] = jnp.broadcast_to(wt, (8, cols))
    turned = nt(eye_of(width, width), cust_ref[...])
    w_ref[0:width, :] = turned.astype(BF16)
    hq = 0.5 * jnp.sum(turned * turned, axis=0, keepdims=True)
    hq_ref[...] = hq
    w_ref[width:, :] = jnp.zeros((width, cols), BF16)
    sel = eye_of(16, width)
    acc[...] = jnp.zeros_like(acc)
    pay[...] = jnp.zeros_like(pay)

    def set_aug(lam):
        a1, a2, a3 = split3(64.0 * lam - hq_ref[...])
        aug = jnp.concatenate([a1.astype(F32), a2.astype(F32), a3.astype(F32), jnp.ones((3, cols), F32),
                               jnp.broadcast_to(-64.0 * d_ref[0:1, :], (3, cols)), jnp.zeros((7, cols), F32)], axis=0)
        w_ref[width:width + 16, :] = aug.astype(BF16)

    def forward_first(b):
        @pl.when(b != f)
        def _():
            for cpy in first_copy(b, f, f):
                cpy.wait_recv()
            for e in range(half - 1):
                for cpy in side_copy(b, e, c):
                    cpy.start()
            for cpy in twin_copy(b, 0, c):
                cpy.start()

    def forward_side(b):
        @pl.when(b != f)
        def _():
            for e in range(half - 1):
                q = lax.rem(c + nc - 2 * (e + 1), nc)
                for cpy in side_copy(b, e, q):
                    cpy.wait_recv()
                for cpy in twin_copy(b, e + 1, q):
                    cpy.start()

    def arrived(b):
        @pl.when(b != f)
        def _():
            for e in range(half):
                for cpy in twin_copy(b, e, rows_from(e)):
                    cpy.wait_recv()

    def rows_from(e):
        return lax.rem(twin[1] + nc - 2 * e, nc)

    def prepare(b, k):
        if k == 0:
            inf = jnp.concatenate([infos[b, p] for p in range(nc)], axis=1)
            mu, cap = inf[1:2], inf[2:3]
            caps[b] = inf
            bias = inf[0:1]
        else:
            g = (k - 1) * nf + b
            wait_second(g)
            inf = caps[b]
            bias, cap = inf[0:1], inf[2:3]
            load = total_of(g)[:, 0:padded]
            mu = mus[b]
            mu = jnp.maximum(0.0, mu + (0.1 / k) * (load - cap) / (load + jnp.where(cap > 0, cap, 1.0)))
        mus[b] = mu
        parts = [p.astype(F32) for p in split3(bias) + split3(mu)]
        stack = jnp.concatenate([jnp.ones((3, padded), F32)] + parts + [jnp.zeros((7, padded), F32)], axis=0).astype(BF16)
        col = lax.dot_general(stack, sel, (((0,), (0,)), ((), ())), preferred_element_type=F32).astype(BF16)
        side[b] = col

    def first_sum(g, e, peer):
        return pltpu.make_async_remote_copy(pay.at[g], got1.at[g, e], s4.at[g], r4.at[g], device_id=peer, device_id_type=MESH)

    def second_sum(g, d, peer):
        return pltpu.make_async_remote_copy(mid.at[g], got2.at[g, d], s5.at[g], r5.at[g], device_id=peer, device_id_type=MESH)

    def all_first(g):
        return pltpu.make_async_remote_copy(got1.at[g], got1.at[g], s4.at[g], r4.at[g], device_id=twin, device_id_type=MESH)

    def all_second(g):
        return pltpu.make_async_remote_copy(got2.at[g], got2.at[g], s5.at[g], r5.at[g], device_id=twin, device_id_type=MESH)

    def wait_second(g):
        all_second(g).wait_recv()

    def total_of(g):
        total = mid[g]
        for d in range(nf - 1):
            total = total + got2[g, d]
        return total

    def pass_on(g):
        all_first(g).wait_recv()
        total = pay[g]
        for e in range(nc - 1):
            total = total + got1[g, e]
        mid[g] = total
        for d in range(1, nf):
            second_sum(g, d - 1, (lax.rem(f + d, nf), c)).start()

    block = y_ref.shape[2]
    tiles = cols // block
    groups = block // 128
    scale = math.log2(math.e) / 6.4

    def dot(b, t, slot):
        lhs = jnp.concatenate([facs[b, 0:rows], side[b, 0:rows]], axis=1)
        y_ref[slot] = jnp.dot(lhs, w_ref[:, t * block:(t + 1) * block], preferred_element_type=F32)

    def tile(t, slot):
        at = [slice(t * block + q * 128, t * block + (q + 1) * 128) for q in range(groups)]
        covs = [cov_ref[:, a] for a in at]
        softs = [soft_ref[:, a] for a in at]
        ds = [d_ref[:, a] for a in at]
        for r in range(0, rows, 32):
            size = min(4, (rows - r) // 8)
            sums = [None] * size
            for q in range(groups):
                es = [jnp.exp2(y_ref[slot, r + 8 * s:r + 8 * s + 8, q * 128:(q + 1) * 128] * scale) for s in range(size)]
                us = [1.0 + e for e in es]
                p01 = us[0] * us[1]
                if size == 4:
                    p23 = us[2] * us[3]
                    p = p01 * p23
                    inv = ds[q] * (1.0 / p)
                    r01, r23 = inv * p23, inv * p01
                    xs = [es[0] * (us[1] * r01), es[1] * (us[0] * r01), es[2] * (us[3] * r23), es[3] * (us[2] * r23)]
                    covs[q] = covs[q] + ((xs[0] + xs[1]) + (xs[2] + xs[3]))
                else:
                    p = p01
                    inv = ds[q] * (1.0 / p)
                    xs = [es[0] * (us[1] * inv), es[1] * (us[0] * inv)]
                    covs[q] = covs[q] + (xs[0] + xs[1])
                softs[q] = softs[q] + jnp.log(p)
                sums = [x if s is None else s + x for s, x in zip(sums, xs)]
            for s in range(size):
                lo = r + 8 * s
                acc[lo:lo + 8, :] = sums[s] if t == 0 else acc[lo:lo + 8, :] + sums[s]
        for q in range(groups):
            cov_ref[:, at[q]] = covs[q]
            soft_ref[:, at[q]] = softs[q]

    set_aug(lam)
    if nf > 1:
        forward_first(0)
        forward_first(1)
        forward_side(0)
        arrived(0)
    ones16 = jnp.ones((16, 128), BF16)

    for k in range(ITERS):
        cov_ref[...] = jnp.zeros_like(cov_ref)
        soft_ref[...] = jnp.zeros_like(soft_ref)
        if k == 0:
            forward_first(2)
            forward_side(1)
        prepare(0, k)
        dot(0, 0, 0)

        def body(b, _, k=k):
            g = k * nf + b
            nxt = lax.rem(b + 1, nf)
            for t in range(tiles - 1):
                dot(b, t + 1, (t + 1) % 2)
                tile(t, t % 2)

            @pl.when(b + 1 < nf)
            def _():
                if k == 0:
                    @pl.when(b + 3 < nf)
                    def _():
                        forward_first(b + 3)

                    @pl.when(b + 2 < nf)
                    def _():
                        forward_side(b + 2)
                    arrived(b + 1)
                prepare(b + 1, k)
            dot(nxt, 0, tiles % 2)
            tile(tiles - 1, (tiles - 1) % 2)
            part_sum = acc[...]
            hi = part_sum.astype(BF16)
            lo = (part_sum - hi.astype(F32)).astype(BF16)
            row = (nt(ones16, hi) + nt(ones16, lo))[0:1]
            pay[g, :, 0:padded] = row
            if k == ITERS - 1:
                @pl.when(b == nf - 1)
                def _():
                    finish_step(k)
            for e in range(nc - 1):
                first_sum(g, e, (f, lax.rem(c + e + 1, nc))).start()

            if k == 0:
                @pl.when(b >= LAG)
                def _():
                    pass_on(g - LAG)
            else:
                pass_on(g - LAG)
            return 0

        def finish_step(k):
            wt = d_ref[0:1, :]
            lam = lam_ref[...]
            cover = jnp.sum(cov_ref[...], axis=0, keepdims=True) / wt
            soft = jnp.sum(soft_ref[...], axis=0, keepdims=True)
            held = jnp.sum(mus[f] * caps[f, 2:3])
            here = jnp.sum(wt * lam - TAU * wt * soft) - jnp.where(c == 0, held, 0.0)
            tot = tot_ref[...] + jnp.where(lane == k, here, 0.0)
            tot_ref[...] = tot
            lam = lam + (0.1 / (k + 1)) * wt * (1.0 - cover) / (1.0 + cover)
            lam_ref[...] = lam
            if k == ITERS - 1:
                pay[ITERS * nf - 1, :, wide - 128:] = tot
            else:
                set_aug(lam)

        lax.fori_loop(0, nf, body, 0)
        if k < ITERS - 1:
            finish_step(k)

    def lam_copy(src, dst, peer_f):
        return pltpu.make_async_remote_copy(lam_ref, lam_out.at[src], s6.at[dst], r6.at[src], device_id=(peer_f, c), device_id_type=MESH)

    for d in range(1, nf):
        peer = lax.rem(f + d, nf)
        lam_copy(f, peer, peer).start()
    lam_out[f] = lam_ref[...]
    last = ITERS * nf

    def flush(i, _):
        pass_on(last - LAG + i)
        return 0

    lax.fori_loop(0, min(LAG, nf), flush, 0)

    def drain(i, _):
        wait_second(last - nf + i)
        return 0

    lax.fori_loop(0, nf, drain, 0)
    load = total_of(last - nf + f)[:, 0:padded]
    inf = caps[f]
    cap = inf[2:3]
    mu = mus[f]
    mu = jnp.maximum(0.0, mu + (0.1 / ITERS) * (load - cap) / (load + jnp.where(cap > 0, cap, 1.0)))
    stack = jnp.concatenate([v.astype(F32) for v in split3(mu)] + [jnp.zeros((13, padded), F32)], axis=0).astype(BF16)
    back = jnp.dot(stack, hot_ref[...], preferred_element_type=F32)
    shut = mu_in_ref[...]
    for k in range(ITERS):
        shut = jnp.maximum(0.0, shut - 0.1 / (k + 1))
    cap_out[...] = jnp.where(open_ref[...] > 0, back[0:1] + back[1:2] + back[2:3], shut)
    bound_out[...] = total_of(last - 1)[:, wide - 128:] / total_cust
    most = jnp.max(jnp.max(caps[:, 3, :], axis=0, keepdims=True), axis=1, keepdims=True)
    flag_out[...] = jnp.broadcast_to((most > rows).astype(jnp.int32), (1, 128))

    def close(j, _):
        src = lax.rem(f + j, nf)
        for cpy in first_copy(f, src, src):
            cpy.wait_send()
        lam_copy(src, src, src).wait()
        for e in range(half - 1):
            for cpy in side_copy(src, e, c):
                cpy.wait_send()
        for e in range(half):
            for cpy in twin_copy(src, e, c):
                cpy.wait_send()
        return 0

    lax.fori_loop(1, nf, close, 0)

    def settle(g, _):
        all_first(g).wait_send()
        all_second(g).wait_send()
        return 0

    lax.fori_loop(0, last, settle, 0)


def local(nf, nc, fac_coords, cust_coords, open_flags, demand, fixed_cost, capacity, cap_mult, cover_mult):
    n, width = fac_coords.shape
    cols = cust_coords.shape[0]
    sd = jax.ShapeDtypeStruct
    dma = pltpu.SemaphoreType.DMA
    half = nc // 2
    open_row = open_flags.reshape(1, n)
    block = math.gcd(cols, 512) if cols > 512 else cols // 2
    args = (open_row, fac_coords, capacity.reshape(1, n), cap_mult.reshape(1, n), fixed_cost.reshape(1, n), cust_coords,
            demand.reshape(1, nf * cols), cover_mult.reshape(1, nf * cols))

    def run(rows, cid):
        part = -(-rows // (16 * nc)) * 16
        padded = part * nc
        wide = -(-padded // 128) * 128 + 128
        last = ITERS * nf
        return pl.pallas_call(
            functools.partial(solve_kernel, nf, nc, rows, cols * nf * nc),
            out_shape=(sd((nf, 1, cols), F32), sd((1, n), F32), sd((1, 128), F32), sd((1, 128), jnp.int32)),
            in_specs=[VMEM] * 8, out_specs=(VMEM,) * 4,
            scratch_shapes=[
                pltpu.VMEM((nf, padded, width), BF16),
                pltpu.VMEM((nf, nc, 8, part), F32),
                pltpu.VMEM((padded, n), BF16),
                pltpu.VMEM((nf, padded, width), BF16),
                pltpu.VMEM((2 * width, cols), BF16),
                pltpu.VMEM((2, rows, block), F32),
                pltpu.VMEM((padded, 128), F32),
                pltpu.VMEM((8, cols), F32),
                pltpu.VMEM((8, cols), F32),
                pltpu.VMEM((8, cols), F32),
                pltpu.VMEM((1, cols), F32),
                pltpu.VMEM((1, cols), F32),
                pltpu.VMEM((nf, 1, padded), F32),
                pltpu.VMEM((nf, 8, padded), F32),
                pltpu.VMEM((1, 128), F32),
                pltpu.VMEM((last, 1, wide), F32),
                pltpu.VMEM((last, nc - 1, 1, wide), F32),
                pltpu.VMEM((last, 1, wide), F32),
                pltpu.VMEM((last, nf - 1, 1, wide), F32),
                dma((nf, 2)), dma((nf, 2)),
                dma((nf, half - 1, 2)), dma((nf, half - 1, 2)),
                dma((nf, half, 2)), dma((nf, half, 2)),
                dma((last,)), dma((last,)), dma((last,)), dma((last,)),
                dma((nf,)), dma((nf,)),
            ],
            compiler_params=pltpu.CompilerParams(collective_id=cid, has_side_effects=True, vmem_limit_bytes=56 * 2 ** 20),
            name="solve",
        )(*args)

    rows = min(n, -(-int(n / 2 + 2 * math.sqrt(n)) // 16) * 16)
    lam, cap, bound, flag = run(rows, 0)
    if rows < n:
        lam, cap, bound = lax.cond(flag[0, 0] > 0, lambda: tuple(run(n, 1)[:3]), lambda: (lam, cap, bound))
    return lam.reshape(nf * cols), cap.reshape(n), bound[0, :ITERS]


def solution(mesh):
    nf, nc = mesh.shape["fac"], mesh.shape["cust"]
    return jax.shard_map(
        functools.partial(local, nf, nc),
        mesh=mesh,
        in_specs=(P("fac", None), P(("cust", "fac"), None), P("fac"), P("cust"), P("fac"), P("fac"), P("fac"), P("cust")),
        out_specs=(P("cust"), P("fac"), P()),
        check_vma=False,
    )
```

time: 115 us -> 73.2 us (0.64)
  Pallas kernels: 113 us -> 69.2 us
  local copies, waits for them, and re-layouts: 1.8 us -> 3.04 us
    pallas_call x9 -> x1, Pallas kernels: 113 us -> 69.2 us  [run(): pl.pallas_call(functools.partial(solve_kernel, nf, nc, rows, cols * nf *...]
    unnamed x5 -> x22, local copies, waits for them, and re-layouts: 1.29 us -> 3.03 us
where the time goes in v1:
time: 73.2 us; the launch traced here: 73 us
  Pallas kernels  69.2 us (95%)
  local copies, waits for them, and re-layouts  3.04 us (4%)
  between operations  0.81 us (1%)
    pallas_call x1, Pallas kernels, run(): pl.pallas_call(functools.partial(solve_kernel, nf, nc, rows, cols * nf *...  69.2 us
    unnamed x22, local copies, waits for them, and re-layouts  3.03 us

profile of v1, /device:TPU:0, one launch (start us, length us, event | category | flops | bytes accessed | tf_op | source)
XLA Modules:
  0.0 73.0 jit_solution(10275107925995242210)
XLA Ops:
  0.6 0.0 copy-start
  0.6 0.0 copy-start.1
  0.7 0.0 copy-start.2
  0.7 0.0 copy-start.3
  0.7 69.2 %solve.3 = (f32[8,1,2048]{2,1,0:T(1,128)S(1)}, f32[1,512]{1,0:T(1,128)S(1)}, f32[1,128]{1,0:T(1,128)S(1)}, s32[1,128]{1,0:T(1,128)}) custom-call(s32[1,512]{1,0:T(1,128)} %bitcast.22, bf16[512,128]{1,0:T(8,128)(2,1)} %fac_ref.1, f32[1,512]{1,0:T(1,128)} %bitcast.24, f32[1,512]{1,0:T(1,128)} %bitcast.26, f32[1,512]{1,0:T(1,128)} %bitcast.28, ...), custom_call_target="tpu_custom_call" | custom-call | tf_op jit(solution)/shard_map/solve/pallas_call | solution.py:414
  69.8 0.0 copy-start.5
  69.8 0.0 copy-start.6
  69.9 0.0 copy-start.7
  69.9 0.0 copy-start.9
  69.9 0.7 copy-done.9
  70.6 0.0 copy-start.4
  70.6 0.0 copy-done
  70.6 0.0 copy-done.1
  70.6 0.0 copy-done.2
  70.6 0.0 copy-done.3
  70.6 0.0 copy-done.5
  70.7 0.0 copy-done.6
  70.7 0.0 copy-done.7
  70.7 0.6 copy-done.4
  71.3 0.0 copy-start.10
  71.3 0.5 copy-done.10
  71.8 0.6 copy.21
  72.4 0.6 copy.22
  (2 shorter events, 0.0 us)
Async XLA Ops:
  0.6 70.0 %copy-start = (bf16[2048,128]{1,0:T(8,128)(2,1)S(1)}, bf16[2048,128]{1,0:T(8,128)(2,1)}, u32[]{:S(2)}) copy-start(bf16[2048,128]{1,0:T(8,128)(2,1)} %cust_ref.1) | copy-start | bytes 1572868
  0.6 70.0 %copy-start.1 = (bf16[512,128]{1,0:T(8,128)(2,1)S(1)}, bf16[512,128]{1,0:T(8,128)(2,1)}, u32[]{:S(2)}) copy-start(bf16[512,128]{1,0:T(8,128)(2,1)} %fac_ref.1) | copy-start | bytes 393220
  0.7 70.0 %copy-start.2 = (s32[16384]{0:T(1024)S(1)}, s32[16384]{0:T(1024)}, u32[]{:S(2)}) copy-start(s32[16384]{0:T(1024)} %param.13) | copy-start | bytes 196612
  0.7 70.0 %copy-start.3 = (f32[16384]{0:T(1024)S(1)}, f32[16384]{0:T(1024)}, u32[]{:S(2)}) copy-start(f32[16384]{0:T(1024)} %param.17) | copy-start | bytes 196612
  69.8 0.8 %copy-start.5 = (f32[512]{0:T(512)S(1)}, f32[512]{0:T(512)}, u32[]{:S(2)}) copy-start(f32[512]{0:T(512)} %param.15) | copy-start | bytes 6148
  69.8 0.8 %copy-start.6 = (f32[512]{0:T(512)S(1)}, f32[512]{0:T(512)}, u32[]{:S(2)}) copy-start(f32[512]{0:T(512)} %param.16) | copy-start | bytes 6148
  69.9 0.8 %copy-start.7 = (f32[512]{0:T(512)S(1)}, f32[512]{0:T(512)}, u32[]{:S(2)}) copy-start(f32[512]{0:T(512)} %param.14) | copy-start | bytes 6148
  69.9 0.7 copy-start.9
  70.6 0.7 copy-start.4
  71.3 0.5 copy-start.10

commit v2 on v1

v2 whole, which is shorter than its diff:
```python
import functools
import math

import jax
import jax.numpy as jnp
from jax import lax
from jax.experimental import pallas as pl
from jax.experimental.pallas import tpu as pltpu
from jax.sharding import PartitionSpec as P

MESH = pl.DeviceIdType.MESH
ITERS = 3
TAU = 0.1
LAG = 3
CLOSED = -30000.0
F32 = jnp.float32
BF16 = jnp.bfloat16
VMEM = pl.BlockSpec(memory_space=pltpu.VMEM)
SMEM = pl.BlockSpec(memory_space=pltpu.SMEM)
HBM = pl.BlockSpec(memory_space=pltpu.HBM)


def split3(v):
    a = v.astype(BF16)
    r = v - a.astype(F32)
    b = r.astype(BF16)
    c = (r - b.astype(F32)).astype(BF16)
    return a, b, c


def nt(a, b):
    return lax.dot_general(a, b, (((1,), (1,)), ((), ())), preferred_element_type=F32)


def eye_of(rows, width):
    hit = lax.broadcasted_iota(jnp.int32, (rows, width), 0) == lax.broadcasted_iota(jnp.int32, (rows, width), 1)
    return hit.astype(F32).astype(BF16)


def onehot_of(open_row, rows):
    n = open_row.shape[1]
    flags = jnp.broadcast_to(open_row.astype(F32), (16, n)).astype(BF16)
    tri = (lax.broadcasted_iota(jnp.int32, (n, n), 0) <= lax.broadcasted_iota(jnp.int32, (n, n), 1)).astype(F32).astype(BF16)
    pos = jnp.dot(flags, tri, preferred_element_type=F32)[0:1]
    pos = jnp.where(open_row > 0, pos - 1.0, -1.0).astype(jnp.int32)
    hit = lax.broadcasted_iota(jnp.int32, (rows, n), 0) == pos
    return jnp.where(hit, 1.0, 0.0).astype(BF16)


def solve_kernel(nf, nc, rows, total_cust,
                 open_in, fac_in, cap_in, mu_in, fixed_in, cust_in, demand_in, cover_in,
                 lam_out, cap_out, bound_out, flag_out,
                 open_ref, fac_ref, cap_ref, mu_in_ref, fixed_ref, cust_ref, demand_ref, cover_ref, loads,
                 facs, infos, hot_ref, side, w_ref, y_ref, acc, cov_ref, soft_ref, d_ref, hq_ref, lam_ref, mus, caps,
                 tot_ref, dl_ref, pay, got1, mid, got2,
                 s1, r1, s2, r2, s3, r3, s4, r4, s5, r5, s6, r6):
    f, c = lax.axis_index("fac"), lax.axis_index("cust")
    n, width = fac_ref.shape
    cols = cust_ref.shape[0]
    part = infos.shape[3]
    padded = part * nc
    wide = pay.shape[2]
    half = nc // 2
    core = lax.rem(c, 2)
    twin = (f, c + 1 - 2 * core)
    barrier = pltpu.get_barrier_semaphore()
    for d in range(1, nf):
        pl.semaphore_signal(barrier, inc=1, device_id=(lax.rem(f + d, nf), c), device_id_type=MESH)
    for d in range(1, nc):
        pl.semaphore_signal(barrier, inc=1, device_id=(f, lax.rem(c + d, nc)), device_id_type=MESH)

    mine = pl.ds(pl.multiple_of(f * cols, cols), cols)
    fetch = [pltpu.make_async_copy(src, dst, loads.at[i]) for i, (src, dst) in enumerate([
        (open_in, open_ref), (fac_in, fac_ref), (cap_in, cap_ref), (mu_in, mu_in_ref),
        (fixed_in, fixed_ref), (cust_in, cust_ref), (demand_in.at[:, mine], demand_ref), (cover_in.at[:, mine], cover_ref)])]
    for cpy in fetch:
        cpy.start()
    for cpy in fetch[:4]:
        cpy.wait()

    opened = open_ref[...].astype(F32)
    hot = onehot_of(open_ref[...], padded)
    hot_ref[...] = hot
    fac = fac_ref[...]
    facs[f] = jnp.dot(hot, fac, preferred_element_type=F32).astype(BF16)
    q1, q2, _ = split3(fac.astype(F32) ** 2)
    ones = jnp.ones((16, width), BF16)
    halfsq = -0.5 * (nt(ones, q1) + nt(ones, q2))[0:1]
    rows16 = [jnp.ones((1, n), BF16)]
    for v in (halfsq, mu_in_ref[...], cap_ref[...]):
        rows16.extend(split3(v))
    rows16 = [r.astype(F32) for r in rows16] + [jnp.zeros((6, n), F32)]
    got = nt(jnp.concatenate(rows16, axis=0).astype(BF16), hot)
    bias = jnp.where(got[0:1] > 0, got[1:2] + got[2:3] + got[3:4], CLOSED)
    count = jnp.broadcast_to(jnp.sum(opened, axis=1, keepdims=True), (1, padded))
    info = jnp.concatenate([bias, got[4:5] + got[5:6] + got[6:7], got[7:8] + got[8:9] + got[9:10], count], axis=0)
    for p in range(nc):
        infos[f, p] = info[:, p * part:(p + 1) * part]

    def rows_of(q):
        return pl.ds(pl.multiple_of(q * part, 16), part)

    def bulk(ref, send, recv):
        return pltpu.make_async_remote_copy(ref, ref, send, recv, device_id=twin, device_id_type=MESH)

    def move(src, q, send, recv, peer):
        a, b = facs.at[src, rows_of(q)], infos.at[src, q]
        return [pltpu.make_async_remote_copy(a, a, send.at[0], recv.at[0], device_id=peer, device_id_type=MESH),
                pltpu.make_async_remote_copy(b, b, send.at[1], recv.at[1], device_id=peer, device_id_type=MESH)]

    def first_copy(src, peer_f):
        return move(src, c, s1, r1.at[src], (peer_f, c))

    def side_copy(src, e, q):
        return move(src, q, s2, r2.at[src, e], (f, lax.rem(c + 2 * (e + 1), nc)))

    def twin_copy(src, q):
        return move(src, q, s3, r3.at[src], twin)

    pl.semaphore_wait(barrier, nf + nc - 2)
    upper = f // (nf // 2)
    for j in range(nf - 1):
        down = nf - 2 - j + (nf - 2 - j + nf - f) // nf
        up = j + (j + nf - f) // nf
        for cpy in first_copy(f, upper * up + (1 - upper) * down):
            cpy.start()

    for cpy in fetch[4:]:
        cpy.wait()
    ext = jnp.zeros((1, 128), F32)
    lane = lax.broadcasted_iota(jnp.int32, (1, 128), 1)
    shut = mu_in_ref[...]
    for k in range(ITERS):
        fixed = jnp.sum(opened * fixed_ref[...] - (1.0 - opened) * shut * cap_ref[...])
        ext = ext + jnp.where((lane == k) & (c == 0), fixed, 0.0)
        shut = jnp.maximum(0.0, shut - 0.1 / (k + 1))
    tot_ref[...] = ext
    wt = demand_ref[...].astype(F32)
    lam = cover_ref[...]
    lam_ref[...] = lam
    d_ref[...] = jnp.broadcast_to(wt, (8, cols))
    turned = nt(eye_of(width, width), cust_ref[...])
    w_ref[0:width, :] = turned.astype(BF16)
    hq = 0.5 * jnp.sum(turned * turned, axis=0, keepdims=True)
    hq_ref[...] = hq
    w_ref[width:, :] = jnp.zeros((width, cols), BF16)
    sel = eye_of(16, width)
    acc[...] = jnp.zeros_like(acc)
    lanes_d = jnp.zeros((1, 128), F32)
    for t in range(cols // 128):
        lanes_d = lanes_d + wt[:, t * 128:(t + 1) * 128]
    dl_ref[...] = lanes_d
    pay[...] = jnp.zeros_like(pay)

    def set_aug(lam):
        a1, a2, a3 = split3(64.0 * lam - hq_ref[...])
        aug = jnp.concatenate([a1.astype(F32), a2.astype(F32), a3.astype(F32), jnp.ones((3, cols), F32),
                               jnp.broadcast_to(-64.0 * d_ref[0:1, :], (3, cols)), jnp.zeros((7, cols), F32)], axis=0)
        w_ref[width:width + 16, :] = aug.astype(BF16)

    def forward_first(b):
        @pl.when(b != f)
        def _():
            for cpy in first_copy(b, f):
                cpy.wait_recv()
            for e in range(half - 1):
                for cpy in side_copy(b, e, c):
                    cpy.start()
            for cpy in twin_copy(b, c):
                cpy.start()

    def forward_side(b):
        @pl.when(b != f)
        def _():
            for e in range(half - 1):
                q = lax.rem(c + nc - 2 * (e + 1), nc)
                for cpy in side_copy(b, e, q):
                    cpy.wait_recv()
                for cpy in twin_copy(b, q):
                    cpy.start()

    def arrived(b):
        @pl.when(b != f)
        def _():
            bulk(facs.at[b, 0:half * part], s3.at[0], r3.at[b, 0]).wait_recv()
            bulk(infos.at[b, 0:half], s3.at[1], r3.at[b, 1]).wait_recv()

    def prepare(b, k):
        if k == 0:
            inf = jnp.concatenate([infos[b, p] for p in range(nc)], axis=1)
            bias, mu = inf[0:1], inf[1:2]
            caps[b] = inf
        else:
            g = (k - 1) * nf + b
            inf = caps[b]
            bias, cap = inf[0:1], inf[2:3]
            load = total_of(g)[:, 0:padded]
            mu = jnp.maximum(0.0, mus[g] + (0.1 / k) * (load - cap) / (load + jnp.where(cap > 0, cap, 1.0)))
        mus[k * nf + b] = mu
        parts = [p.astype(F32) for p in split3(bias) + split3(mu)]
        stack = jnp.concatenate([jnp.ones((3, padded), F32)] + parts + [jnp.zeros((7, padded), F32)], axis=0).astype(BF16)
        side[b] = lax.dot_general(stack, sel, (((0,), (0,)), ((), ())), preferred_element_type=F32).astype(BF16)

    def first_sum(g, e, peer):
        return pltpu.make_async_remote_copy(pay.at[g], got1.at[g, e], s4, r4.at[g], device_id=peer, device_id_type=MESH)

    def second_sum(g, d, peer):
        return pltpu.make_async_remote_copy(mid.at[g], got2.at[g, d], s5, r5.at[g], device_id=peer, device_id_type=MESH)

    def wait_second(g):
        bulk(got2.at[g], s5, r5.at[g]).wait_recv()

    def total_of(g):
        total = mid[g]
        for d in range(nf - 1):
            total = total + got2[g, d]
        return total

    def pass_on(g):
        bulk(got1.at[g], s4, r4.at[g]).wait_recv()
        total = pay[g]
        for e in range(nc - 1):
            total = total + got1[g, e]
        mid[g] = total
        for d in range(1, nf):
            second_sum(g, d - 1, (lax.rem(f + d, nf), c)).start()

    block = y_ref.shape[2]
    tiles = cols // block
    groups = block // 128
    scale = math.log2(math.e) / 6.4

    def dot(b, t, slot):
        lhs = jnp.concatenate([facs[b, 0:rows], side[b, 0:rows]], axis=1)
        y_ref[slot] = jnp.dot(lhs, w_ref[:, t * block:(t + 1) * block], preferred_element_type=F32)

    def tile(b, t, slot):
        at = [slice(t * block + q * 128, t * block + (q + 1) * 128) for q in range(groups)]
        covs = [cov_ref[:, a] for a in at]
        softs = [soft_ref[:, a] for a in at]
        ds = [d_ref[:, a] for a in at]
        for r in range(0, rows, 32):
            size = min(4, (rows - r) // 8)
            sums = [None] * size
            for q in range(groups):
                us = [1.0 + jnp.exp2(y_ref[slot, r + 8 * s:r + 8 * s + 8, q * 128:(q + 1) * 128] * scale) for s in range(size)]
                gs = []
                p = None
                for s in range(0, size, 2):
                    pair = us[s] * us[s + 1]
                    inv = ds[q] * (1.0 / pair)
                    gs += [us[s + 1] * inv, us[s] * inv]
                    p = pair if p is None else p * pair
                held = gs[0] + gs[1]
                if size == 4:
                    held = held + (gs[2] + gs[3])
                covs[q] = covs[q] + (float(size) * ds[q] - held)
                softs[q] = softs[q] + jnp.log2(p)
                sums = [g if v is None else v + g for v, g in zip(sums, gs)]
            for s in range(size):
                lo = r + 8 * s
                acc[b, lo:lo + 8, :] = sums[s] if t == 0 else acc[b, lo:lo + 8, :] + sums[s]
        for q in range(groups):
            cov_ref[:, at[q]] = covs[q]
            soft_ref[:, at[q]] = softs[q]

    ones16 = jnp.ones((16, 128), BF16)
    live = lax.broadcasted_iota(jnp.int32, (padded, 128), 0) < rows

    def row_of(b, g):
        part_sum = jnp.where(live, dl_ref[...] - acc[b], 0.0)
        hi = part_sum.astype(BF16)
        lo = (part_sum - hi.astype(F32)).astype(BF16)
        pay[g, :, 0:padded] = (nt(ones16, hi) + nt(ones16, lo))[0:1]

    def send_row(g):
        for e in range(nc - 1):
            first_sum(g, e, (f, lax.rem(c + e + 1, nc))).start()

    pair = f - lax.rem(f, 2)

    def place(k, p):
        if k > 0:
            return p
        q = p - 2
        far = q + 2 * ((q + nf - pair) // nf)
        return jnp.where(p == 0, f, jnp.where(p == 1, 2 * pair + 1 - f, far))

    def finish_step(k):
        wt = d_ref[0:1, :]
        lam = lam_ref[...]
        cover = jnp.sum(cov_ref[...], axis=0, keepdims=True) / wt
        soft = math.log(2.0) * jnp.sum(soft_ref[...], axis=0, keepdims=True)
        held = jnp.sum(mus[k * nf + f] * caps[f, 2:3])
        here = jnp.sum(wt * lam - TAU * wt * soft) - jnp.where(c == 0, held, 0.0)
        tot = tot_ref[...] + jnp.where(lane == k, here, 0.0)
        tot_ref[...] = tot
        lam = lam + (0.1 / (k + 1)) * wt * (1.0 - cover) / (1.0 + cover)
        lam_ref[...] = lam
        if k == ITERS - 1:
            pay[ITERS * nf - 1, :, wide - 128:] = tot
        else:
            set_aug(lam)

    def gather_turn(p):
        for i in range(3):
            at = 3 * p - 1 + i

            @pl.when((at > 0) & (at < nf))
            def _():
                forward_first(place(0, at))

        @pl.when(p < 2)
        def _():
            forward_side(place(0, p + 1))

        @pl.when((p > 0) & (p + 2 < nf))
        def _():
            forward_side(place(0, p + 2))

        @pl.when(p + 1 < nf)
        def _():
            arrived(place(0, p + 1))

    set_aug(lam)
    for k in range(ITERS):
        cov_ref[...] = jnp.zeros_like(cov_ref)
        soft_ref[...] = jnp.zeros_like(soft_ref)
        start = f if k == 0 else 0
        if k > 0:
            wait_second((k - 1) * nf)
        prepare(start, k)
        dot(start, 0, 0)

        def body(p, _, k=k):
            b = place(k, p)
            nxt = place(k, lax.rem(p + 1, nf))
            if k == 0:
                before = place(0, lax.rem(p + nf - 1, nf))
            elif k == 1:
                before = jnp.where(p == 0, place(0, nf - 1), nf + p - 1)
            else:
                before = k * nf + p - 1
            if k == 0:
                row_of(before, before)
            else:
                row_of(lax.rem(before, nf), before)
            for t in range(tiles // 2):
                dot(b, t + 1, (t + 1) % 2)
                tile(b, t, t % 2)
            if k == 0:
                @pl.when(p > 0)
                def _():
                    send_row(before)

                @pl.when(p >= LAG)
                def _():
                    pass_on(place(0, p - LAG))
                gather_turn(p)
            else:
                send_row(before)
                if k == 1:
                    pass_on(jnp.where(p < LAG, place(0, nf + p - LAG), nf + p - LAG))
                else:
                    pass_on(k * nf + p - LAG)

                @pl.when(p + 1 < nf)
                def _():
                    wait_second((k - 1) * nf + p + 1)
            for t in range(tiles // 2, tiles - 1):
                dot(b, t + 1, (t + 1) % 2)
                tile(b, t, t % 2)
            prepare(nxt, k)
            dot(nxt, 0, tiles % 2)
            tile(b, tiles - 1, (tiles - 1) % 2)
            return 0

        lax.fori_loop(0, nf, body, 0)
        finish_step(k)

    last = ITERS * nf
    row_of(nf - 1, last - 1)
    send_row(last - 1)

    for d in range(1, nf):
        pltpu.make_async_remote_copy(lam_ref, lam_out.at[f], s6, r6, device_id=(lax.rem(f + d, nf), c), device_id_type=MESH).start()
    lam_out[f] = lam_ref[...]
    for send, recv, width_parts in ((s1, r1, 1), (s2, r2, half - 1), (s3, r3, half)):
        bulk(facs.at[0:nf - 1, 0:width_parts * part], send.at[0], recv.at[(0,) * (len(recv.shape) - 1) + (0,)]).wait_send()
        bulk(infos.at[0:nf - 1, 0:width_parts], send.at[1], recv.at[(0,) * (len(recv.shape) - 1) + (1,)]).wait_send()

    def flush(i, _):
        pass_on(last - LAG + i)
        return 0

    lax.fori_loop(0, LAG, flush, 0)

    def drain(i, _):
        wait_second(last - nf + i)
        return 0

    lax.fori_loop(0, nf, drain, 0)
    load = total_of(last - nf + f)[:, 0:padded]
    inf = caps[f]
    cap = inf[2:3]
    mu = mus[last - nf + f]
    mu = jnp.maximum(0.0, mu + (0.1 / ITERS) * (load - cap) / (load + jnp.where(cap > 0, cap, 1.0)))
    stack = jnp.concatenate([v.astype(F32) for v in split3(mu)] + [jnp.zeros((13, padded), F32)], axis=0).astype(BF16)
    back = jnp.dot(stack, hot_ref[...], preferred_element_type=F32)
    shut = mu_in_ref[...]
    for k in range(ITERS):
        shut = jnp.maximum(0.0, shut - 0.1 / (k + 1))
    cap_out[...] = jnp.where(open_ref[...] > 0, back[0:1] + back[1:2] + back[2:3], shut)
    bound_out[...] = total_of(last - 1)[:, wide - 128:] / total_cust
    most = jnp.max(jnp.max(caps[:, 3, :], axis=0, keepdims=True), axis=1, keepdims=True)
    flag_out[0, 0] = (most[0, 0] > rows).astype(jnp.int32)

    lams = bulk(lam_out.at[0:nf - 1], s6, r6)
    lams.wait_send()
    lams.wait_recv()
    bulk(got1, s4, r4.at[0]).wait_send()
    bulk(got2, s5, r5.at[0]).wait_send()


def finish_kernel(lam_ref, cap_ref, bound_ref, lam_out, cap_out, bound_out):
    lam_out[...] = lam_ref[...]
    cap_out[...] = cap_ref[...]
    bound_out[...] = bound_ref[:, 0:bound_out.shape[1]]


def local(nf, nc, fac_coords, cust_coords, open_flags, demand, fixed_cost, capacity, cap_mult, cover_mult):
    n, width = fac_coords.shape
    cols = cust_coords.shape[0]
    sd = jax.ShapeDtypeStruct
    dma = pltpu.SemaphoreType.DMA
    half = nc // 2
    open_row = open_flags.reshape(1, n)
    block = math.gcd(cols, 256)
    args = (open_row, fac_coords, capacity.reshape(1, n), cap_mult.reshape(1, n), fixed_cost.reshape(1, n), cust_coords,
            demand.reshape(1, nf * cols), cover_mult.reshape(1, nf * cols))

    def run(rows, cid):
        part = -(-rows // (16 * nc)) * 16
        padded = part * nc
        wide = -(-padded // 128) * 128 + 128
        last = ITERS * nf
        return pl.pallas_call(
            functools.partial(solve_kernel, nf, nc, rows, cols * nf * nc),
            out_shape=(sd((nf, 1, cols), F32), sd((1, n), F32), sd((1, 128), F32), sd((1, 1), jnp.int32)),
            in_specs=[HBM] * 8, out_specs=(VMEM,) * 3 + (SMEM,),
            scratch_shapes=[
                pltpu.VMEM((1, n), jnp.int32),
                pltpu.VMEM((n, width), BF16),
                pltpu.VMEM((1, n), F32),
                pltpu.VMEM((1, n), F32),
                pltpu.VMEM((1, n), F32),
                pltpu.VMEM((cols, width), BF16),
                pltpu.VMEM((1, cols), jnp.int32),
                pltpu.VMEM((1, cols), F32),
                dma((8,)),
                pltpu.VMEM((nf, padded, width), BF16),
                pltpu.VMEM((nf, nc, 4, part), F32),
                pltpu.VMEM((padded, n), BF16),
                pltpu.VMEM((nf, padded, width), BF16),
                pltpu.VMEM((2 * width, cols), BF16),
                pltpu.VMEM((2, rows, block), F32),
                pltpu.VMEM((nf, padded, 128), F32),
                pltpu.VMEM((8, cols), F32),
                pltpu.VMEM((8, cols), F32),
                pltpu.VMEM((8, cols), F32),
                pltpu.VMEM((1, cols), F32),
                pltpu.VMEM((1, cols), F32),
                pltpu.VMEM((last, 1, padded), F32),
                pltpu.VMEM((nf, 4, padded), F32),
                pltpu.VMEM((1, 128), F32),
                pltpu.VMEM((1, 128), F32),
                pltpu.VMEM((last, 1, wide), F32),
                pltpu.VMEM((last, nc - 1, 1, wide), F32),
                pltpu.VMEM((last, 1, wide), F32),
                pltpu.VMEM((last, nf - 1, 1, wide), F32),
                dma((2,)), dma((nf, 2)),
                dma((2,)), dma((nf, half - 1, 2)),
                dma((2,)), dma((nf, 2)),
                dma(()), dma((last,)), dma(()), dma((last,)),
                dma(()), dma(()),
            ],
            compiler_params=pltpu.CompilerParams(collective_id=cid, has_side_effects=True, vmem_limit_bytes=56 * 2 ** 20),
            name="solve",
        )(*args)

    rows = min(n, -(-int(n / 2 + 2 * math.sqrt(n)) // 16) * 16)
    lam, cap, bound, flag = run(rows, 0)
    if rows < n:
        lam, cap, bound = lax.cond(flag[0, 0] > 0, lambda: tuple(run(n, 1)[:3]), lambda: (lam, cap, bound))
    lam, cap, bound = pl.pallas_call(
        finish_kernel, out_shape=(sd((nf, 1, cols), F32), sd((1, n), F32), sd((1, ITERS), F32)),
        in_specs=[VMEM] * 3, out_specs=(VMEM,) * 3, name="finish",
    )(lam, cap, bound)
    return lam.reshape(nf * cols), cap.reshape(n), bound.reshape(ITERS)


def solution(mesh):
    nf, nc = mesh.shape["fac"], mesh.shape["cust"]
    return jax.shard_map(
        functools.partial(local, nf, nc),
        mesh=mesh,
        in_specs=(P("fac", None), P(("cust", "fac"), None), P("fac"), P("cust"), P("fac"), P("fac"), P("fac"), P("cust")),
        out_specs=(P("cust"), P("fac"), P()),
        check_vma=False,
    )
```

time: 73.2 us -> 59.3 us (0.81)
  Pallas kernels: 69.2 us -> 57.1 us
  local copies, waits for them, and re-layouts: 3.04 us -> 0.66 us
    pallas_call x1, Pallas kernels: 69.2 us -> 56.5 us  [run(): pl.pallas_call(functools.partial(solve_kernel, nf, nc, rows, cols * nf *...]
    unnamed x22 -> x16, local copies, waits for them, and re-layouts: 3.03 us -> 0.66 us
where the time goes in v2:
time: 59.3 us; the launch traced here: 59.1 us
  Pallas kernels  57.1 us (96%)
  between operations  1.32 us (2%)
  local copies, waits for them, and re-layouts  0.66 us (1%)
    pallas_call x1, Pallas kernels, run(): pl.pallas_call(functools.partial(solve_kernel, nf, nc, rows, cols * nf *...  56.5 us

profile of v2, /device:TPU:0, one launch (start us, length us, event | category | flops | bytes accessed | tf_op | source)
XLA Modules:
  0.0 59.1 jit_solution(3400502223824000110)
XLA Ops:
  0.6 0.0 copy-start
  0.6 0.0 copy-start.1
  0.7 0.0 copy-start.2
  0.7 0.0 copy-start.3
  0.7 56.5 %solve.3 = (f32[8,1,2048]{2,1,0:T(1,128)S(1)}, f32[1,512]{1,0:T(1,128)S(1)}, f32[1,128]{1,0:T(1,128)S(1)}, s32[1,1]{1,0:T(1,128)}) custom-call(s32[1,512]{1,0:T(1,128)} %bitcast.14, bf16[512,128]{1,0:T(8,128)(2,1)} %fac_in.1, f32[1,512]{1,0:T(1,128)} %bitcast.16, f32[1,512]{1,0:T(1,128)} %bitcast.18, f32[1,512]{1,0:T(1,128)} %bitcast.20, ...), custom_call_target="tpu_custom_call" | custom-call | tf_op jit(solution)/shard_map/solve/pallas_call | solution.py:447
  57.2 0.0 copy-start.5
  57.2 0.0 copy-start.6
  57.2 0.0 copy-start.7
  57.8 0.0 copy-start.4
  57.8 0.0 copy-done
  57.8 0.0 copy-done.1
  57.8 0.0 copy-done.2
  57.8 0.0 copy-done.3
  57.8 0.0 copy-done.5
  57.9 0.0 copy-done.6
  57.9 0.0 copy-done.7
  57.9 0.6 copy-done.4
  58.5 0.6 %finish.1 = (f32[8,1,2048]{2,1,0:T(1,128)}, f32[1,512]{1,0:T(1,128)}, f32[1,3]{1,0:T(1,128)}) custom-call(f32[8,1,2048]{2,1,0:T(1,128)S(1)} %get-tuple-element.50.lam_ref, f32[1,512]{1,0:T(1,128)S(1)} %get-tuple-element.51.cap_ref, f32[1,128]{1,0:T(1,128)S(1)} %get-tuple-element.52.bound_ref), custom_call_target="tpu_custom_call" | custom-call | tf_op jit(solution)/shard_map/finish/pallas_call | solution.py:495
  (1 shorter events, 0.0 us)
Async XLA Ops:
  0.6 57.2 %copy-start = (bf16[2048,128]{1,0:T(8,128)(2,1)S(1)}, bf16[2048,128]{1,0:T(8,128)(2,1)}, u32[]{:S(2)}) copy-start(bf16[2048,128]{1,0:T(8,128)(2,1)} %cust_in.1) | copy-start | bytes 1572868
  0.6 57.2 %copy-start.1 = (bf16[512,128]{1,0:T(8,128)(2,1)S(1)}, bf16[512,128]{1,0:T(8,128)(2,1)}, u32[]{:S(2)}) copy-start(bf16[512,128]{1,0:T(8,128)(2,1)} %fac_in.1) | copy-start | bytes 393220
  0.7 57.2 %copy-start.2 = (s32[16384]{0:T(1024)S(1)}, s32[16384]{0:T(1024)}, u32[]{:S(2)}) copy-start(s32[16384]{0:T(1024)} %param.13) | copy-start | bytes 196612
  0.7 57.2 %copy-start.3 = (f32[16384]{0:T(1024)S(1)}, f32[16384]{0:T(1024)}, u32[]{:S(2)}) copy-start(f32[16384]{0:T(1024)} %param.17) | copy-start | bytes 196612
  57.2 0.7 %copy-start.5 = (f32[512]{0:T(512)S(1)}, f32[512]{0:T(512)}, u32[]{:S(2)}) copy-start(f32[512]{0:T(512)} %param.15) | copy-start | bytes 6148
  57.2 0.7 %copy-start.6 = (f32[512]{0:T(512)S(1)}, f32[512]{0:T(512)}, u32[]{:S(2)}) copy-start(f32[512]{0:T(512)} %param.16) | copy-start | bytes 6148
  57.2 0.7 %copy-start.7 = (f32[512]{0:T(512)S(1)}, f32[512]{0:T(512)}, u32[]{:S(2)}) copy-start(f32[512]{0:T(512)} %param.14) | copy-start | bytes 6148
  57.8 0.7 %copy-start.4 = (s32[512]{0:T(512)S(1)}, s32[512]{0:T(512)}, u32[]{:S(2)}) copy-start(s32[512]{0:T(512)} %param.12) | copy-start | bytes 6148

commit v3 on v2

--- a/solution.py
+++ b/solution.py
@@ -48,12 +48,15 @@
 
 
 def solve_kernel(nf, nc, rows, total_cust,
-                 open_in, fac_in, cap_in, mu_in, fixed_in, cust_in, demand_in, cover_in,
-                 lam_out, cap_out, bound_out, flag_out,
-                 open_ref, fac_ref, cap_ref, mu_in_ref, fixed_ref, cust_ref, demand_ref, cover_ref, loads,
+                 first, *refs):
+    small_in, (fac_in, cust_in, demand_in, cover_in), refs = (refs[:4], refs[4:8], refs[8:]) if first else (refs[0], refs[1:5], refs[5:])
+    (lam_out, cap_out, bound_out), refs = refs[:3], refs[3:]
+    if first:
+        (flag_out, small_out), refs = refs[:2], refs[2:]
+    (open_ref, fac_ref, cap_ref, mu_in_ref, fixed_ref, cust_ref, demand_ref, cover_ref, loads,
                  facs, infos, hot_ref, side, w_ref, y_ref, acc, cov_ref, soft_ref, d_ref, hq_ref, lam_ref, mus, caps,
                  tot_ref, dl_ref, pay, got1, mid, got2,
-                 s1, r1, s2, r2, s3, r3, s4, r4, s5, r5, s6, r6):
+                 s1, r1, s2, r2, s3, r3, s4, r4, s5, r5, s6, r6) = refs
     f, c = lax.axis_index("fac"), lax.axis_index("cust")
     n, width = fac_ref.shape
     cols = cust_ref.shape[0]
@@ -66,17 +69,27 @@
     barrier = pltpu.get_barrier_semaphore()
     for d in range(1, nf):
         pl.semaphore_signal(barrier, inc=1, device_id=(lax.rem(f + d, nf), c), device_id_type=MESH)
+        pl.semaphore_signal(barrier, inc=1, device_id=(lax.rem(f + d, nf), twin[1]), device_id_type=MESH)
     for d in range(1, nc):
         pl.semaphore_signal(barrier, inc=1, device_id=(f, lax.rem(c + d, nc)), device_id_type=MESH)
 
     mine = pl.ds(pl.multiple_of(f * cols, cols), cols)
-    fetch = [pltpu.make_async_copy(src, dst, loads.at[i]) for i, (src, dst) in enumerate([
-        (open_in, open_ref), (fac_in, fac_ref), (cap_in, cap_ref), (mu_in, mu_in_ref),
-        (fixed_in, fixed_ref), (cust_in, cust_ref), (demand_in.at[:, mine], demand_ref), (cover_in.at[:, mine], cover_ref)])]
+    pairs = [(fac_in, fac_ref), (cust_in, cust_ref), (demand_in.at[:, mine], demand_ref), (cover_in.at[:, mine], cover_ref)]
+    if first:
+        pairs += list(zip(small_in, (open_ref, cap_ref, mu_in_ref, fixed_ref)))
+    fetch = [pltpu.make_async_copy(src, dst, loads.at[i]) for i, (src, dst) in enumerate(pairs)]
     for cpy in fetch:
         cpy.start()
-    for cpy in fetch[:4]:
+    for cpy in fetch[:1] + fetch[4:]:
         cpy.wait()
+    if first:
+        small_out[0:1, :] = open_ref[...].astype(F32)
+        for i, ref in enumerate((cap_ref, mu_in_ref, fixed_ref)):
+            small_out[i + 1:i + 2, :] = ref[...]
+    else:
+        open_ref[...] = small_in[0:1, :].astype(jnp.int32)
+        for i, ref in enumerate((cap_ref, mu_in_ref, fixed_ref)):
+            ref[...] = small_in[i + 1:i + 2, :]
 
     opened = open_ref[...].astype(F32)
     hot = onehot_of(open_ref[...], padded)
@@ -108,8 +121,8 @@
         return [pltpu.make_async_remote_copy(a, a, send.at[0], recv.at[0], device_id=peer, device_id_type=MESH),
                 pltpu.make_async_remote_copy(b, b, send.at[1], recv.at[1], device_id=peer, device_id_type=MESH)]
 
-    def first_copy(src, peer_f):
-        return move(src, c, s1, r1.at[src], (peer_f, c))
+    def first_copy(src, peer_f, peer_c):
+        return move(src, peer_c, s1, r1.at[src], (peer_f, peer_c))
 
     def side_copy(src, e, q):
         return move(src, q, s2, r2.at[src, e], (f, lax.rem(c + 2 * (e + 1), nc)))
@@ -117,15 +130,19 @@
     def twin_copy(src, q):
         return move(src, q, s3, r3.at[src], twin)
 
-    pl.semaphore_wait(barrier, nf + nc - 2)
+    pl.semaphore_wait(barrier, 2 * (nf - 1) + nc - 1)
     upper = f // (nf // 2)
-    for j in range(nf - 1):
-        down = nf - 2 - j + (nf - 2 - j + nf - f) // nf
-        up = j + (j + nf - f) // nf
-        for cpy in first_copy(f, upper * up + (1 - upper) * down):
-            cpy.start()
-
-    for cpy in fetch[4:]:
+
+    @pl.when(core == 1)
+    def _():
+        for j in range(nf - 1):
+            down = nf - 2 - j + (nf - 2 - j + nf - f) // nf
+            up = j + (j + nf - f) // nf
+            for peer_c in (c - 1, c):
+                for cpy in first_copy(f, upper * up + (1 - upper) * down, peer_c):
+                    cpy.start()
+
+    for cpy in fetch[1:4]:
         cpy.wait()
     ext = jnp.zeros((1, 128), F32)
     lane = lax.broadcasted_iota(jnp.int32, (1, 128), 1)
@@ -161,7 +178,7 @@
     def forward_first(b):
         @pl.when(b != f)
         def _():
-            for cpy in first_copy(b, f):
+            for cpy in first_copy(b, f, c):
                 cpy.wait_recv()
             for e in range(half - 1):
                 for cpy in side_copy(b, e, c):
@@ -227,11 +244,12 @@
 
     block = y_ref.shape[2]
     tiles = cols // block
+    tall = y_ref.shape[1]
     groups = block // 128
     scale = math.log2(math.e) / 6.4
 
     def dot(b, t, slot):
-        lhs = jnp.concatenate([facs[b, 0:rows], side[b, 0:rows]], axis=1)
+        lhs = jnp.concatenate([facs[b, 0:tall], side[b, 0:tall]], axis=1)
         y_ref[slot] = jnp.dot(lhs, w_ref[:, t * block:(t + 1) * block], preferred_element_type=F32)
 
     def tile(b, t, slot):
@@ -246,12 +264,17 @@
                 us = [1.0 + jnp.exp2(y_ref[slot, r + 8 * s:r + 8 * s + 8, q * 128:(q + 1) * 128] * scale) for s in range(size)]
                 gs = []
                 p = None
-                for s in range(0, size, 2):
-                    pair = us[s] * us[s + 1]
-                    inv = ds[q] * (1.0 / pair)
+                for s in range(0, size - 1, 2):
+                    two = us[s] * us[s + 1]
+                    inv = ds[q] * (1.0 / two)
                     gs += [us[s + 1] * inv, us[s] * inv]
-                    p = pair if p is None else p * pair
-                held = gs[0] + gs[1]
+                    p = two if p is None else p * two
+                if size % 2:
+                    gs.append(ds[q] * (1.0 / us[-1]))
+                    p = us[-1] if p is None else p * us[-1]
+                held = gs[0] if size == 1 else gs[0] + gs[1]
+                if size == 3:
+                    held = held + gs[2]
                 if size == 4:
                     held = held + (gs[2] + gs[3])
                 covs[q] = covs[q] + (float(size) * ds[q] - held)
@@ -303,20 +326,21 @@
             set_aug(lam)
 
     def gather_turn(p):
-        for i in range(3):
-            at = 3 * p - 1 + i
-
-            @pl.when((at > 0) & (at < nf))
-            def _():
-                forward_first(place(0, at))
-
-        @pl.when(p < 2)
+        @pl.when(p == 0)
         def _():
-            forward_side(place(0, p + 1))
-
-        @pl.when((p > 0) & (p + 2 < nf))
+            forward_first(place(0, 1))
+            forward_side(place(0, 1))
+
+            def each(i, _):
+                forward_first(place(0, i))
+                return 0
+
+            lax.fori_loop(2, nf, each, 0)
+
+        @pl.when((p > 0) & (2 * p < nf))
         def _():
-            forward_side(place(0, p + 2))
+            forward_side(place(0, 2 * p))
+            forward_side(place(0, 2 * p + 1))
 
         @pl.when(p + 1 < nf)
         def _():
@@ -385,7 +409,13 @@
     for d in range(1, nf):
         pltpu.make_async_remote_copy(lam_ref, lam_out.at[f], s6, r6, device_id=(lax.rem(f + d, nf), c), device_id_type=MESH).start()
     lam_out[f] = lam_ref[...]
-    for send, recv, width_parts in ((s1, r1, 1), (s2, r2, half - 1), (s3, r3, half)):
+
+    @pl.when(core == 1)
+    def _():
+        bulk(facs.at[0:nf - 1, 0:2 * part], s1.at[0], r1.at[0, 0]).wait_send()
+        bulk(infos.at[0:nf - 1, 0:2], s1.at[1], r1.at[0, 1]).wait_send()
+
+    for send, recv, width_parts in ((s2, r2, half - 1), (s3, r3, half)):
         bulk(facs.at[0:nf - 1, 0:width_parts * part], send.at[0], recv.at[(0,) * (len(recv.shape) - 1) + (0,)]).wait_send()
         bulk(infos.at[0:nf - 1, 0:width_parts], send.at[1], recv.at[(0,) * (len(recv.shape) - 1) + (1,)]).wait_send()
 
@@ -412,8 +442,9 @@
         shut = jnp.maximum(0.0, shut - 0.1 / (k + 1))
     cap_out[...] = jnp.where(open_ref[...] > 0, back[0:1] + back[1:2] + back[2:3], shut)
     bound_out[...] = total_of(last - 1)[:, wide - 128:] / total_cust
-    most = jnp.max(jnp.max(caps[:, 3, :], axis=0, keepdims=True), axis=1, keepdims=True)
-    flag_out[0, 0] = (most[0, 0] > rows).astype(jnp.int32)
+    if first:
+        most = jnp.max(jnp.max(caps[:, 3, :], axis=0, keepdims=True), axis=1, keepdims=True)
+        flag_out[0, 0] = (most[0, 0] > rows).astype(jnp.int32)
 
     lams = bulk(lam_out.at[0:nf - 1], s6, r6)
     lams.wait_send()
@@ -436,18 +467,20 @@
     half = nc // 2
     open_row = open_flags.reshape(1, n)
     block = math.gcd(cols, 256)
-    args = (open_row, fac_coords, capacity.reshape(1, n), cap_mult.reshape(1, n), fixed_cost.reshape(1, n), cust_coords,
-            demand.reshape(1, nf * cols), cover_mult.reshape(1, nf * cols))
-
-    def run(rows, cid):
+    small = (open_row, capacity.reshape(1, n), cap_mult.reshape(1, n), fixed_cost.reshape(1, n))
+    large = (fac_coords, cust_coords, demand.reshape(1, nf * cols), cover_mult.reshape(1, nf * cols))
+
+    def run(rows, cid, packed=None):
         part = -(-rows // (16 * nc)) * 16
         padded = part * nc
         wide = -(-padded // 128) * 128 + 128
         last = ITERS * nf
+        first = packed is None
         return pl.pallas_call(
-            functools.partial(solve_kernel, nf, nc, rows, cols * nf * nc),
-            out_shape=(sd((nf, 1, cols), F32), sd((1, n), F32), sd((1, 128), F32), sd((1, 1), jnp.int32)),
-            in_specs=[HBM] * 8, out_specs=(VMEM,) * 3 + (SMEM,),
+            functools.partial(solve_kernel, nf, nc, rows, cols * nf * nc, first),
+            out_shape=(sd((nf, 1, cols), F32), sd((1, n), F32), sd((1, 128), F32)) + ((sd((1, 1), jnp.int32), sd((4, n), F32)) if first else ()),
+            in_specs=[HBM] * 8 if first else [VMEM] + [HBM] * 4,
+            out_specs=(VMEM,) * 3 + ((SMEM, VMEM) if first else ()),
             scratch_shapes=[
                 pltpu.VMEM((1, n), jnp.int32),
                 pltpu.VMEM((n, width), BF16),
@@ -463,7 +496,7 @@
                 pltpu.VMEM((padded, n), BF16),
                 pltpu.VMEM((nf, padded, width), BF16),
                 pltpu.VMEM((2 * width, cols), BF16),
-                pltpu.VMEM((2, rows, block), F32),
+                pltpu.VMEM((2, -(-rows // 16) * 16, block), F32),
                 pltpu.VMEM((nf, padded, 128), F32),
                 pltpu.VMEM((8, cols), F32),
                 pltpu.VMEM((8, cols), F32),
@@ -486,12 +519,12 @@
             ],
             compiler_params=pltpu.CompilerParams(collective_id=cid, has_side_effects=True, vmem_limit_bytes=56 * 2 ** 20),
             name="solve",
-        )(*args)
-
-    rows = min(n, -(-int(n / 2 + 2 * math.sqrt(n)) // 16) * 16)
-    lam, cap, bound, flag = run(rows, 0)
+        )(*(small if first else (packed,)), *large)
+
+    rows = min(n, -(-int(n / 2 + 1.75 * math.sqrt(n)) // 8) * 8)
+    lam, cap, bound, flag, packed = run(rows, 0)
     if rows < n:
-        lam, cap, bound = lax.cond(flag[0, 0] > 0, lambda: tuple(run(n, 1)[:3]), lambda: (lam, cap, bound))
+        lam, cap, bound = lax.cond(flag[0, 0] > 0, lambda: tuple(run(n, 1, packed)), lambda: (lam, cap, bound))
     lam, cap, bound = pl.pallas_call(
         finish_kernel, out_shape=(sd((nf, 1, cols), F32), sd((1, n), F32), sd((1, ITERS), F32)),
         in_specs=[VMEM] * 3, out_specs=(VMEM,) * 3, name="finish",

time: 59.3 us -> 55.3 us (0.933)
  Pallas kernels: 57.1 us -> 53.5 us
  local copies, waits for them, and re-layouts: 0.66 us -> 0.02 us
    pallas_call x1, Pallas kernels: 56.5 us -> 52.9 us  [run(): pl.pallas_call(functools.partial(solve_kernel, nf, nc, rows, cols * nf *...]
    unnamed x16 -> x8, local copies, waits for them, and re-layouts: 0.66 us -> 0.02 us
where the time goes in v3:
time: 55.3 us; the launch traced here: 55.2 us
  Pallas kernels  53.5 us (97%)
  between operations  1.4 us (3%)
    pallas_call x1, Pallas kernels, run(): pl.pallas_call(functools.partial(solve_kernel, nf, nc, rows, cols * nf *...  52.9 us

profile of v3, /device:TPU:0, one launch (start us, length us, event | category | flops | bytes accessed | tf_op | source)
XLA Modules:
  0.0 55.2 jit_solution(17325894289308339250)
XLA Ops:
  0.6 0.0 copy-start
  0.6 0.0 copy-start.1
  0.7 0.0 copy-start.2
  0.7 0.0 copy-start.3
  0.7 52.9 %solve.3 = (f32[8,1,2048]{2,1,0:T(1,128)S(1)}, f32[1,512]{1,0:T(1,128)S(1)}, f32[1,128]{1,0:T(1,128)S(1)}, s32[1,1]{1,0:T(1,128)}, f32[4,512]{1,0:T(4,128)S(1)}) custom-call(s32[1,512]{1,0:T(1,128)} %bitcast.14, f32[1,512]{1,0:T(1,128)} %bitcast.15, f32[1,512]{1,0:T(1,128)} %bitcast.16, f32[1,512]{1,0:T(1,128)} %bitcast.17, bf16[512,128]{1,0:T(8,128)(2,1)} %refs_4_.1, ...), custom_call_target="tpu_custom_call" | custom-call | tf_op jit(solution)/shard_map/solve/pallas_call | solution.py:479
  54.2 0.0 copy-done
  54.3 0.0 copy-done.1
  54.3 0.0 copy-done.2
  54.3 0.0 copy-done.3
  54.3 0.2 conditional.1
  54.5 0.6 %finish.1 = (f32[8,1,2048]{2,1,0:T(1,128)}, f32[1,512]{1,0:T(1,128)}, f32[1,3]{1,0:T(1,128)}) custom-call(f32[8,1,2048]{2,1,0:T(1,128)S(1)} %get-tuple-element.40.lam_ref, f32[1,512]{1,0:T(1,128)S(1)} %get-tuple-element.41.cap_ref, f32[1,128]{1,0:T(1,128)S(1)} %get-tuple-element.42.bound_ref), custom_call_target="tpu_custom_call" | custom-call | tf_op jit(solution)/shard_map/finish/pallas_call | solution.py:528
Async XLA Ops:
  0.6 53.6 %copy-start = (bf16[2048,128]{1,0:T(8,128)(2,1)S(1)}, bf16[2048,128]{1,0:T(8,128)(2,1)}, u32[]{:S(2)}) copy-start(bf16[2048,128]{1,0:T(8,128)(2,1)} %refs_5_.1) | copy-start | bytes 1572868
  0.6 53.6 %copy-start.1 = (bf16[512,128]{1,0:T(8,128)(2,1)S(1)}, bf16[512,128]{1,0:T(8,128)(2,1)}, u32[]{:S(2)}) copy-start(bf16[512,128]{1,0:T(8,128)(2,1)} %refs_4_.1) | copy-start | bytes 393220
  0.7 53.6 %copy-start.2 = (s32[16384]{0:T(1024)S(1)}, s32[16384]{0:T(1024)}, u32[]{:S(2)}) copy-start(s32[16384]{0:T(1024)} %param.13) | copy-start | bytes 196612
  0.7 53.6 %copy-start.3 = (f32[16384]{0:T(1024)S(1)}, f32[16384]{0:T(1024)}, u32[]{:S(2)}) copy-start(f32[16384]{0:T(1024)} %param.17) | copy-start | bytes 196612

commit v4 on v3

--- a/solution.py
+++ b/solution.py
@@ -261,25 +261,28 @@
             size = min(4, (rows - r) // 8)
             sums = [None] * size
             for q in range(groups):
-                us = [1.0 + jnp.exp2(y_ref[slot, r + 8 * s:r + 8 * s + 8, q * 128:(q + 1) * 128] * scale) for s in range(size)]
-                gs = []
+                es = [jnp.exp2(y_ref[slot, r + 8 * s:r + 8 * s + 8, q * 128:(q + 1) * 128] * scale) for s in range(size)]
+                xs = []
                 p = None
                 for s in range(0, size - 1, 2):
-                    two = us[s] * us[s + 1]
+                    both = es[s] * es[s + 1]
+                    left, right = es[s] + both, es[s + 1] + both
+                    two = (1.0 + es[s]) + right
                     inv = ds[q] * (1.0 / two)
-                    gs += [us[s + 1] * inv, us[s] * inv]
+                    xs += [left * inv, right * inv]
                     p = two if p is None else p * two
                 if size % 2:
-                    gs.append(ds[q] * (1.0 / us[-1]))
-                    p = us[-1] if p is None else p * us[-1]
-                held = gs[0] if size == 1 else gs[0] + gs[1]
+                    one = 1.0 + es[-1]
+                    xs.append(es[-1] * (ds[q] * (1.0 / one)))
+                    p = one if p is None else p * one
+                total = xs[0] if size == 1 else xs[0] + xs[1]
                 if size == 3:
-                    held = held + gs[2]
+                    total = total + xs[2]
                 if size == 4:
-                    held = held + (gs[2] + gs[3])
-                covs[q] = covs[q] + (float(size) * ds[q] - held)
+                    total = total + (xs[2] + xs[3])
+                covs[q] = covs[q] + total
                 softs[q] = softs[q] + jnp.log2(p)
-                sums = [g if v is None else v + g for v, g in zip(sums, gs)]
+                sums = [x if v is None else v + x for v, x in zip(sums, xs)]
             for s in range(size):
                 lo = r + 8 * s
                 acc[b, lo:lo + 8, :] = sums[s] if t == 0 else acc[b, lo:lo + 8, :] + sums[s]
@@ -288,10 +291,9 @@
             soft_ref[:, at[q]] = softs[q]
 
     ones16 = jnp.ones((16, 128), BF16)
-    live = lax.broadcasted_iota(jnp.int32, (padded, 128), 0) < rows
 
     def row_of(b, g):
-        part_sum = jnp.where(live, dl_ref[...] - acc[b], 0.0)
+        part_sum = acc[b]
         hi = part_sum.astype(BF16)
         lo = (part_sum - hi.astype(F32)).astype(BF16)
         pay[g, :, 0:padded] = (nt(ones16, hi) + nt(ones16, lo))[0:1]

time: 55.3 us -> 55.4 us (level)
  no operation moved by 1% of the time
where the time goes in v4:
time: 55.4 us; the launch traced here: 55.2 us
  Pallas kernels  53.6 us (97%)
  between operations  1.4 us (3%)
    pallas_call x1, Pallas kernels, run(): pl.pallas_call(functools.partial(solve_kernel, nf, nc, rows, cols * nf *...  52.9 us

profile of v4, /device:TPU:0, one launch (start us, length us, event | category | flops | bytes accessed | tf_op | source)
XLA Modules:
  0.0 55.2 jit_solution(16514542734125945071)
XLA Ops:
  0.6 0.0 copy-start
  0.6 0.0 copy-start.1
  0.7 0.0 copy-start.2
  0.7 0.0 copy-start.3
  0.7 52.9 %solve.3 = (f32[8,1,2048]{2,1,0:T(1,128)S(1)}, f32[1,512]{1,0:T(1,128)S(1)}, f32[1,128]{1,0:T(1,128)S(1)}, s32[1,1]{1,0:T(1,128)}, f32[4,512]{1,0:T(4,128)S(1)}) custom-call(s32[1,512]{1,0:T(1,128)} %bitcast.14, f32[1,512]{1,0:T(1,128)} %bitcast.15, f32[1,512]{1,0:T(1,128)} %bitcast.16, f32[1,512]{1,0:T(1,128)} %bitcast.17, bf16[512,128]{1,0:T(8,128)(2,1)} %refs_4_.1, ...), custom_call_target="tpu_custom_call" | custom-call | tf_op jit(solution)/shard_map/solve/pallas_call | solution.py:481
  54.3 0.0 copy-done
  54.3 0.0 copy-done.1
  54.3 0.0 copy-done.2
  54.3 0.0 copy-done.3
  54.3 0.2 conditional.1
  54.6 0.6 %finish.1 = (f32[8,1,2048]{2,1,0:T(1,128)}, f32[1,512]{1,0:T(1,128)}, f32[1,3]{1,0:T(1,128)}) custom-call(f32[8,1,2048]{2,1,0:T(1,128)S(1)} %get-tuple-element.40.lam_ref, f32[1,512]{1,0:T(1,128)S(1)} %get-tuple-element.41.cap_ref, f32[1,128]{1,0:T(1,128)S(1)} %get-tuple-element.42.bound_ref), custom_call_target="tpu_custom_call" | custom-call | tf_op jit(solution)/shard_map/finish/pallas_call | solution.py:530
Async XLA Ops:
  0.6 53.7 %copy-start = (bf16[2048,128]{1,0:T(8,128)(2,1)S(1)}, bf16[2048,128]{1,0:T(8,128)(2,1)}, u32[]{:S(2)}) copy-start(bf16[2048,128]{1,0:T(8,128)(2,1)} %refs_5_.1) | copy-start | bytes 1572868
  0.6 53.7 %copy-start.1 = (bf16[512,128]{1,0:T(8,128)(2,1)S(1)}, bf16[512,128]{1,0:T(8,128)(2,1)}, u32[]{:S(2)}) copy-start(bf16[512,128]{1,0:T(8,128)(2,1)} %refs_4_.1) | copy-start | bytes 393220
  0.7 53.7 %copy-start.2 = (s32[16384]{0:T(1024)S(1)}, s32[16384]{0:T(1024)}, u32[]{:S(2)}) copy-start(s32[16384]{0:T(1024)} %param.13) | copy-start | bytes 196612
  0.7 53.7 %copy-start.3 = (f32[16384]{0:T(1024)S(1)}, f32[16384]{0:T(1024)}, u32[]{:S(2)}) copy-start(f32[16384]{0:T(1024)} %param.17) | copy-start | bytes 196612
